TPU v7x, 256 devices: a whole 4x4x8 slice. The times are simulated.
256 devices in a mesh: wide: 16 (over y, x_hi, core), narrow: 16 (over x_lo, z).
Axes of the slice: x: 4 (x_hi: 2, x_lo: 2; x = x_hi * 2 + x_lo), y: 4, z: 8, core: 2. Of those that a mesh axis runs over, the one named last changes fastest.
Arguments:
- left: bfloat16 [32, 32, 2048], P('narrow', None, 'wide'), may hold values from -6 to 6
- right: bfloat16 [32, 32, 2048], P('wide', None, 'narrow'), may hold values from -6 to 6
- out_weight: bfloat16 [1024, 128], replicated, may hold values from -1 to 1
- out_bias: float32 [128], replicated, may hold values from -3 to 3
- cotangent: bfloat16 [2048, 2048, 128], P('wide', 'narrow'), may hold values from -0.5 to 0.5
Outputs:
- pair_update: bfloat16 [2048, 2048, 128], P('wide', 'narrow')
- grad_left: float32 [32, 32, 2048], P('narrow', None, 'wide')
- grad_right: float32 [32, 32, 2048], P('wide', None, 'narrow')
All inputs are finite; a program needn't handle non-finite values.
Results may differ from a plain program's by a relative error of at most 0.0045.
Values may be sent and summed in bfloat16 or wider, within the bound.
A program may use at most 64 MiB of HBM per device.

v0:
```python
import math

import jax
import jax.numpy as jnp
from jax import lax
from jax.sharding import PartitionSpec as P


def laid_out(blocks, dim):
    shape = list(blocks.shape[1:])
    shape[dim] *= blocks.shape[0]
    return jnp.moveaxis(blocks, 0, dim).reshape(shape)


def copy_for_each(value, axis):
    copies = jnp.broadcast_to(value, (lax.axis_size(axis), *value.shape))
    return lax.all_to_all(copies, axis, split_axis=0, concat_axis=0, tiled=True)


def collect(value, axis, dim):
    return laid_out(copy_for_each(value, axis), dim)


def cut_along(value, dim, peers):
    shape = value.shape
    blocks = value.reshape(*shape[:dim], peers, shape[dim] // peers, *shape[dim + 1 :])
    return jnp.moveaxis(blocks, dim, 0)


def summed_on_arrival(value, axis, dim):
    blocks = cut_along(value, dim, lax.axis_size(axis))
    arrived = lax.all_to_all(blocks, axis, split_axis=0, concat_axis=0, tiled=True)
    return arrived.sum(axis=0)


def local(left, right, out_weight, out_bias, cotangent):
    left_complete = collect(left, "narrow", 0)
    right_full = collect(right, "wide", 0)
    alignment_rows = left_complete.shape[0]
    channel_count = left_complete.shape[1]
    tile_rows = left_complete.shape[2]
    tile_columns = right_full.shape[2]
    pair_width = cotangent.shape[2]
    rows_per_block = math.gcd(16, tile_rows)
    total_block_count = tile_rows // rows_per_block

    def block_step(block_index, carry):
        running, pairs, grads = carry
        start = (block_index * rows_per_block).astype(jnp.int32)
        left_block = lax.dynamic_slice_in_dim(left_complete, start, rows_per_block, 2)
        cot_block = lax.dynamic_slice_in_dim(cotangent, start, rows_per_block, 0)
        outer_sum = (
            jnp.einsum("sci,sej->ijce", left_block, right_full, preferred_element_type=jnp.float32)
            / alignment_rows
        )
        outer_flat = outer_sum.astype(jnp.bfloat16).reshape(
            rows_per_block * tile_columns, channel_count * channel_count
        )
        pair_out = jnp.dot(outer_flat, out_weight, preferred_element_type=jnp.float32) + out_bias
        pair_out = pair_out.astype(jnp.bfloat16).reshape(rows_per_block, tile_columns, pair_width)
        cot_flat = cot_block.reshape(rows_per_block * tile_columns, pair_width)
        d_outer = lax.dot_general(
            cot_flat, out_weight, (((1,), (1,)), ((), ())), preferred_element_type=jnp.float32
        )
        d_outer = d_outer.astype(jnp.bfloat16).reshape(
            rows_per_block, tile_columns, channel_count, channel_count
        )
        grad_block = (
            jnp.einsum("ijce,sej->sci", d_outer, right_full, preferred_element_type=jnp.float32)
            / alignment_rows
        )
        running = (
            running
            + jnp.einsum("ijce,sci->sej", d_outer, left_block, preferred_element_type=jnp.float32)
            / alignment_rows
        )
        pairs = lax.dynamic_update_slice_in_dim(pairs, pair_out, start, 0)
        grads = lax.dynamic_update_slice_in_dim(grads, grad_block, start, 2)
        return (running, pairs, grads)

    starting_value = (
        jnp.zeros((alignment_rows, channel_count, tile_columns), jnp.float32),
        jnp.zeros((tile_rows, tile_columns, pair_width), jnp.bfloat16),
        jnp.zeros((alignment_rows, channel_count, tile_rows), jnp.float32),
    )
    right_terms, pair_update, grad_terms = lax.fori_loop(
        0, total_block_count, block_step, starting_value
    )
    grad_left = summed_on_arrival(grad_terms, "narrow", 0)
    grad_right = summed_on_arrival(right_terms, "wide", 0)
    return (pair_update, grad_left, grad_right)


def solution(mesh):
    return jax.shard_map(
        local,
        mesh=mesh,
        in_specs=(
            P("narrow", None, "wide"),
            P("wide", None, "narrow"),
            P(),
            P(),
            P("wide", "narrow", None),
        ),
        out_specs=(P("wide", "narrow", None), P("narrow", None, "wide"), P("wide", None, "narrow")),
        check_vma=False,
    )
```

profile of v0, /device:TPU:1, one launch (start us, length us, event | category | flops | bytes accessed | tf_op | source)
XLA Modules:
  0.0 298.8 jit_solution(3200406797028317262)
XLA Ops:
  1.6 16.9 %all_to_all.20 = bf16[16,2,32,128]{3,1,2,0:T(2,128)(2,1)S(1)} all-to-all(bf16[16,2,32,128]{3,1,2,0:T(2,128)(2,1)S(1)} %broadcast_in_dim.14), channel_id=1, replica_groups=mesh['wide'=16,'narrow'=16] {'wide'}, dimensions={0} | all-to-all | bytes 524288 | tf_op jit(solution)/shard_map/all_to_all | solution.py:17
  20.0 8.3 %all-to-all-start = ((bf16[16,2,32,128]{3,2,1,0:T(8,128)(2,1)}), bf16[16,2,32,128]{3,2,1,0:T(8,128)(2,1)S(1)}, u32[]{:S(2)}, u32[]{:S(2)}) async-start(bf16[16,2,32,128]{3,2,1,0:T(8,128)(2,1)} %broadcast_in_dim.13), calls=%async_computation | async-start | bytes 524288 | tf_op jit(solution)/shard_map/all_to_all | solution.py:17
  28.5 7.7 %all-to-all-done = bf16[16,2,32,128]{3,2,1,0:T(8,128)(2,1)S(1)} async-done(((bf16[16,2,32,128]{3,2,1,0:T(8,128)(2,1)}), bf16[16,2,32,128]{3,2,1,0:T(8,128)(2,1)S(1)}, u32[]{:S(2)}, u32[]{:S(2)}) %all-to-all-start) | async-done | bytes 262176 | tf_op jit(solution)/shard_map/all_to_all | solution.py:17
  36.2 2.4 copy.33
  38.6 3.1 %broadcast_in_dim.12 = bf16[128,128,128]{2,1,0:T(8,128)(2,1)} broadcast(bf16[]{:T(256)} %constant.49.clone.1), dimensions={} | broadcast | bytes 4194306 | tf_op jit(solution)/shard_map/broadcast_in_dim | solution.py:83
  41.9 220.0 %while.18 = (s32[]{:T(128)}, f32[32,32,128]{2,0,1:T(8,128)S(1)}, bf16[128,128,128]{2,1,0:T(8,128)(2,1)}, f32[32,32,128]{0,2,1:T(8,128)S(1)}, bf16[32,32,128]{1,0...) while((s32[]{:T(128)}, f32[32,32,128]{2,0,1:T(8,128)S(1)}, ...), condition=%wide.region_1.0_spmd.clone, body=%wide.region_0.0_spmd.clone.sunk | while | flops 1483620352 | bytes 60228316 | solution.py:86
  44.2 2.0 fusion.57
  48.1 3.2 %convolution_convert_fusion.2 = bf16[2048,1024]{1,0:T(8,128)(2,1)} fusion(bf16[2048,128]{1,0:T(8,128)(2,1)S(1)} %bitcast.102, bf16[1024,128]{1,0:T(8,128)(2,1)S(1)} %get-tuple-element.327), kind=kOutput, calls=%fused_computation.6.clone.1 | convolution fusion | flops 538968064 | bytes 4980736 | tf_op jit(solution)/shard_map/while/body/eval_jaxpr/dot_general | solution.py:62
  51.3 6.5 %copy.76 = bf16[2048,1024]{0,1:T(8,128)(2,1)} copy(bf16[2048,1024]{1,0:T(8,128)(2,1)} %convolution_convert_fusion.2) | data formatting | bytes 8388608 | tf_op jit(solution)/shard_map/while/body/eval_jaxpr/convert_element_type | solution.py:65
  57.8 3.6 %copy.77 = bf16[128,8,16,128]{3,2,1,0:T(8,128)(2,1)S(1)} copy(bf16[128,8,16,128]{3,1,2,0:T(8,128)(2,1)} %bitcast.101) | data formatting | bytes 8388608 | tf_op jit(solution)/shard_map/while
  64.6 4.8 %fusion.58 = f32[32,32,128]{2,0,1:T(8,128)S(1)} fusion(bf16[32,32,16,1]{1,0,2,3:T(8,128)(2,1)S(1)} %dynamic-slice_bitcast_fusion.2, bf16[16,128,32,32]{1,0,3,2:T(8,128)(2,1)} %bitcast.104, f32[32,32,128]{2,0,1:T(8,128)S(1)} %get-tuple-element.309, pred[]{:T(512)S(6)} %compare.3), kind=kOutput, calls=%fused_computation.12.clone.1 | convolution fusion | flops 134610944 | bytes 5275649 | tf_op jit(solution)/shard_map/while/body/eval_jaxpr/ijce,sci->sej/dot_general | solution.py:74
  71.7 2.0 fusion.57
  75.6 3.2 %convolution_convert_fusion.2 = bf16[2048,1024]{1,0:T(8,128)(2,1)} fusion(bf16[2048,128]{1,0:T(8,128)(2,1)S(1)} %bitcast.102, bf16[1024,128]{1,0:T(8,128)(2,1)S(1)} %get-tuple-element.327), kind=kOutput, calls=%fused_computation.6.clone.1 | convolution fusion | flops 538968064 | bytes 4980736 | tf_op jit(solution)/shard_map/while/body/eval_jaxpr/dot_general | solution.py:62
  78.8 6.5 %copy.76 = bf16[2048,1024]{0,1:T(8,128)(2,1)} copy(bf16[2048,1024]{1,0:T(8,128)(2,1)} %convolution_convert_fusion.2) | data formatting | bytes 8388608 | tf_op jit(solution)/shard_map/while/body/eval_jaxpr/convert_element_type | solution.py:65
  85.3 3.6 %copy.77 = bf16[128,8,16,128]{3,2,1,0:T(8,128)(2,1)S(1)} copy(bf16[128,8,16,128]{3,1,2,0:T(8,128)(2,1)} %bitcast.101) | data formatting | bytes 8388608 | tf_op jit(solution)/shard_map/while
  92.1 4.8 %fusion.58 = f32[32,32,128]{2,0,1:T(8,128)S(1)} fusion(bf16[32,32,16,1]{1,0,2,3:T(8,128)(2,1)S(1)} %dynamic-slice_bitcast_fusion.2, bf16[16,128,32,32]{1,0,3,2:T(8,128)(2,1)} %bitcast.104, f32[32,32,128]{2,0,1:T(8,128)S(1)} %get-tuple-element.309, pred[]{:T(512)S(6)} %compare.3), kind=kOutput, calls=%fused_computation.12.clone.1 | convolution fusion | flops 134610944 | bytes 5275649 | tf_op jit(solution)/shard_map/while/body/eval_jaxpr/ijce,sci->sej/dot_general | solution.py:74
  99.2 2.0 fusion.57
  103.1 3.2 %convolution_convert_fusion.2 = bf16[2048,1024]{1,0:T(8,128)(2,1)} fusion(bf16[2048,128]{1,0:T(8,128)(2,1)S(1)} %bitcast.102, bf16[1024,128]{1,0:T(8,128)(2,1)S(1)} %get-tuple-element.327), kind=kOutput, calls=%fused_computation.6.clone.1 | convolution fusion | flops 538968064 | bytes 4980736 | tf_op jit(solution)/shard_map/while/body/eval_jaxpr/dot_general | solution.py:62
  106.3 6.5 %copy.76 = bf16[2048,1024]{0,1:T(8,128)(2,1)} copy(bf16[2048,1024]{1,0:T(8,128)(2,1)} %convolution_convert_fusion.2) | data formatting | bytes 8388608 | tf_op jit(solution)/shard_map/while/body/eval_jaxpr/convert_element_type | solution.py:65
  112.8 3.6 %copy.77 = bf16[128,8,16,128]{3,2,1,0:T(8,128)(2,1)S(1)} copy(bf16[128,8,16,128]{3,1,2,0:T(8,128)(2,1)} %bitcast.101) | data formatting | bytes 8388608 | tf_op jit(solution)/shard_map/while
  119.6 4.8 %fusion.58 = f32[32,32,128]{2,0,1:T(8,128)S(1)} fusion(bf16[32,32,16,1]{1,0,2,3:T(8,128)(2,1)S(1)} %dynamic-slice_bitcast_fusion.2, bf16[16,128,32,32]{1,0,3,2:T(8,128)(2,1)} %bitcast.104, f32[32,32,128]{2,0,1:T(8,128)S(1)} %get-tuple-element.309, pred[]{:T(512)S(6)} %compare.3), kind=kOutput, calls=%fused_computation.12.clone.1 | convolution fusion | flops 134610944 | bytes 5275649 | tf_op jit(solution)/shard_map/while/body/eval_jaxpr/ijce,sci->sej/dot_general | solution.py:74
  126.7 2.0 fusion.57
  130.6 3.2 %convolution_convert_fusion.2 = bf16[2048,1024]{1,0:T(8,128)(2,1)} fusion(bf16[2048,128]{1,0:T(8,128)(2,1)S(1)} %bitcast.102, bf16[1024,128]{1,0:T(8,128)(2,1)S(1)} %get-tuple-element.327), kind=kOutput, calls=%fused_computation.6.clone.1 | convolution fusion | flops 538968064 | bytes 4980736 | tf_op jit(solution)/shard_map/while/body/eval_jaxpr/dot_general | solution.py:62
  133.8 6.5 %copy.76 = bf16[2048,1024]{0,1:T(8,128)(2,1)} copy(bf16[2048,1024]{1,0:T(8,128)(2,1)} %convolution_convert_fusion.2) | data formatting | bytes 8388608 | tf_op jit(solution)/shard_map/while/body/eval_jaxpr/convert_element_type | solution.py:65
  140.3 3.6 %copy.77 = bf16[128,8,16,128]{3,2,1,0:T(8,128)(2,1)S(1)} copy(bf16[128,8,16,128]{3,1,2,0:T(8,128)(2,1)} %bitcast.101) | data formatting | bytes 8388608 | tf_op jit(solution)/shard_map/while
  147.1 4.8 %fusion.58 = f32[32,32,128]{2,0,1:T(8,128)S(1)} fusion(bf16[32,32,16,1]{1,0,2,3:T(8,128)(2,1)S(1)} %dynamic-slice_bitcast_fusion.2, bf16[16,128,32,32]{1,0,3,2:T(8,128)(2,1)} %bitcast.104, f32[32,32,128]{2,0,1:T(8,128)S(1)} %get-tuple-element.309, pred[]{:T(512)S(6)} %compare.3), kind=kOutput, calls=%fused_computation.12.clone.1 | convolution fusion | flops 134610944 | bytes 5275649 | tf_op jit(solution)/shard_map/while/body/eval_jaxpr/ijce,sci->sej/dot_general | solution.py:74
  154.2 2.0 fusion.57
  158.1 3.2 %convolution_convert_fusion.2 = bf16[2048,1024]{1,0:T(8,128)(2,1)} fusion(bf16[2048,128]{1,0:T(8,128)(2,1)S(1)} %bitcast.102, bf16[1024,128]{1,0:T(8,128)(2,1)S(1)} %get-tuple-element.327), kind=kOutput, calls=%fused_computation.6.clone.1 | convolution fusion | flops 538968064 | bytes 4980736 | tf_op jit(solution)/shard_map/while/body/eval_jaxpr/dot_general | solution.py:62
  161.3 6.5 %copy.76 = bf16[2048,1024]{0,1:T(8,128)(2,1)} copy(bf16[2048,1024]{1,0:T(8,128)(2,1)} %convolution_convert_fusion.2) | data formatting | bytes 8388608 | tf_op jit(solution)/shard_map/while/body/eval_jaxpr/convert_element_type | solution.py:65
  167.8 3.6 %copy.77 = bf16[128,8,16,128]{3,2,1,0:T(8,128)(2,1)S(1)} copy(bf16[128,8,16,128]{3,1,2,0:T(8,128)(2,1)} %bitcast.101) | data formatting | bytes 8388608 | tf_op jit(solution)/shard_map/while
  174.6 4.8 %fusion.58 = f32[32,32,128]{2,0,1:T(8,128)S(1)} fusion(bf16[32,32,16,1]{1,0,2,3:T(8,128)(2,1)S(1)} %dynamic-slice_bitcast_fusion.2, bf16[16,128,32,32]{1,0,3,2:T(8,128)(2,1)} %bitcast.104, f32[32,32,128]{2,0,1:T(8,128)S(1)} %get-tuple-element.309, pred[]{:T(512)S(6)} %compare.3), kind=kOutput, calls=%fused_computation.12.clone.1 | convolution fusion | flops 134610944 | bytes 5275649 | tf_op jit(solution)/shard_map/while/body/eval_jaxpr/ijce,sci->sej/dot_general | solution.py:74
  181.7 2.0 fusion.57
  185.6 3.2 %convolution_convert_fusion.2 = bf16[2048,1024]{1,0:T(8,128)(2,1)} fusion(bf16[2048,128]{1,0:T(8,128)(2,1)S(1)} %bitcast.102, bf16[1024,128]{1,0:T(8,128)(2,1)S(1)} %get-tuple-element.327), kind=kOutput, calls=%fused_computation.6.clone.1 | convolution fusion | flops 538968064 | bytes 4980736 | tf_op jit(solution)/shard_map/while/body/eval_jaxpr/dot_general | solution.py:62
  188.8 6.5 %copy.76 = bf16[2048,1024]{0,1:T(8,128)(2,1)} copy(bf16[2048,1024]{1,0:T(8,128)(2,1)} %convolution_convert_fusion.2) | data formatting | bytes 8388608 | tf_op jit(solution)/shard_map/while/body/eval_jaxpr/convert_element_type | solution.py:65
  195.3 3.6 %copy.77 = bf16[128,8,16,128]{3,2,1,0:T(8,128)(2,1)S(1)} copy(bf16[128,8,16,128]{3,1,2,0:T(8,128)(2,1)} %bitcast.101) | data formatting | bytes 8388608 | tf_op jit(solution)/shard_map/while
  202.1 4.8 %fusion.58 = f32[32,32,128]{2,0,1:T(8,128)S(1)} fusion(bf16[32,32,16,1]{1,0,2,3:T(8,128)(2,1)S(1)} %dynamic-slice_bitcast_fusion.2, bf16[16,128,32,32]{1,0,3,2:T(8,128)(2,1)} %bitcast.104, f32[32,32,128]{2,0,1:T(8,128)S(1)} %get-tuple-element.309, pred[]{:T(512)S(6)} %compare.3), kind=kOutput, calls=%fused_computation.12.clone.1 | convolution fusion | flops 134610944 | bytes 5275649 | tf_op jit(solution)/shard_map/while/body/eval_jaxpr/ijce,sci->sej/dot_general | solution.py:74
  213.1 3.2 %convolution_convert_fusion.2 = bf16[2048,1024]{1,0:T(8,128)(2,1)} fusion(bf16[2048,128]{1,0:T(8,128)(2,1)S(1)} %bitcast.102, bf16[1024,128]{1,0:T(8,128)(2,1)S(1)} %get-tuple-element.327), kind=kOutput, calls=%fused_computation.6.clone.1 | convolution fusion | flops 538968064 | bytes 4980736 | tf_op jit(solution)/shard_map/while/body/eval_jaxpr/dot_general | solution.py:62
  216.3 6.5 %copy.76 = bf16[2048,1024]{0,1:T(8,128)(2,1)} copy(bf16[2048,1024]{1,0:T(8,128)(2,1)} %convolution_convert_fusion.2) | data formatting | bytes 8388608 | tf_op jit(solution)/shard_map/while/body/eval_jaxpr/convert_element_type | solution.py:65
  222.8 3.6 %copy.77 = bf16[128,8,16,128]{3,2,1,0:T(8,128)(2,1)S(1)} copy(bf16[128,8,16,128]{3,1,2,0:T(8,128)(2,1)} %bitcast.101) | data formatting | bytes 8388608 | tf_op jit(solution)/shard_map/while
  229.6 4.8 %fusion.58 = f32[32,32,128]{2,0,1:T(8,128)S(1)} fusion(bf16[32,32,16,1]{1,0,2,3:T(8,128)(2,1)S(1)} %dynamic-slice_bitcast_fusion.2, bf16[16,128,32,32]{1,0,3,2:T(8,128)(2,1)} %bitcast.104, f32[32,32,128]{2,0,1:T(8,128)S(1)} %get-tuple-element.309, pred[]{:T(512)S(6)} %compare.3), kind=kOutput, calls=%fused_computation.12.clone.1 | convolution fusion | flops 134610944 | bytes 5275649 | tf_op jit(solution)/shard_map/while/body/eval_jaxpr/ijce,sci->sej/dot_general | solution.py:74
  240.6 3.2 %convolution_convert_fusion.2 = bf16[2048,1024]{1,0:T(8,128)(2,1)} fusion(bf16[2048,128]{1,0:T(8,128)(2,1)S(1)} %bitcast.102, bf16[1024,128]{1,0:T(8,128)(2,1)S(1)} %get-tuple-element.327), kind=kOutput, calls=%fused_computation.6.clone.1 | convolution fusion | flops 538968064 | bytes 4980736 | tf_op jit(solution)/shard_map/while/body/eval_jaxpr/dot_general | solution.py:62
  243.8 6.5 %copy.76 = bf16[2048,1024]{0,1:T(8,128)(2,1)} copy(bf16[2048,1024]{1,0:T(8,128)(2,1)} %convolution_convert_fusion.2) | data formatting | bytes 8388608 | tf_op jit(solution)/shard_map/while/body/eval_jaxpr/convert_element_type | solution.py:65
  250.3 3.6 %copy.77 = bf16[128,8,16,128]{3,2,1,0:T(8,128)(2,1)S(1)} copy(bf16[128,8,16,128]{3,1,2,0:T(8,128)(2,1)} %bitcast.101) | data formatting | bytes 8388608 | tf_op jit(solution)/shard_map/while
  257.1 4.8 %fusion.58 = f32[32,32,128]{2,0,1:T(8,128)S(1)} fusion(bf16[32,32,16,1]{1,0,2,3:T(8,128)(2,1)S(1)} %dynamic-slice_bitcast_fusion.2, bf16[16,128,32,32]{1,0,3,2:T(8,128)(2,1)} %bitcast.104, f32[32,32,128]{2,0,1:T(8,128)S(1)} %get-tuple-element.309, pred[]{:T(512)S(6)} %compare.3), kind=kOutput, calls=%fused_computation.12.clone.1 | convolution fusion | flops 134610944 | bytes 5275649 | tf_op jit(solution)/shard_map/while/body/eval_jaxpr/ijce,sci->sej/dot_general | solution.py:74
  263.0 6.7 %all-to-all-start.3 = ((f32[16,2,32,128]{3,1,2,0:T(2,128)}), f32[16,2,32,128]{3,1,2,0:T(2,128)S(1)}, u32[]{:S(2)}, u32[]{:S(2)}) async-start(f32[16,2,32,128]{3,1,2,0:T(2,128)} %copy.37), calls=%async_computation.3 | async-start | bytes 1048576 | tf_op jit(solution)/shard_map/all_to_all | solution.py:32
  271.1 9.7 %all-to-all-done.3 = f32[16,2,32,128]{3,1,2,0:T(2,128)S(1)} async-done(((f32[16,2,32,128]{3,1,2,0:T(2,128)}), f32[16,2,32,128]{3,1,2,0:T(2,128)S(1)}, u32[]{:S(2)}, u32[]{:S(2)}) %all-to-all-start.3) | async-done | bytes 524320 | tf_op jit(solution)/shard_map/all_to_all | solution.py:32
  280.8 4.2 %all-to-all-start.2 = ((f32[16,2,32,128]{3,2,1,0:T(8,128)}), f32[16,2,32,128]{3,2,1,0:T(8,128)S(1)}, u32[]{:S(2)}, u32[]{:S(2)}) async-start(f32[16,2,32,128]{3,2,1,0:T(8,128)} %bitcast.2), calls=%async_computation.2 | async-start | bytes 1048576 | tf_op jit(solution)/shard_map/all_to_all | solution.py:32
  285.8 12.3 %all-to-all-done.2 = f32[16,2,32,128]{3,2,1,0:T(8,128)S(1)} async-done(((f32[16,2,32,128]{3,2,1,0:T(8,128)}), f32[16,2,32,128]{3,2,1,0:T(8,128)S(1)}, u32[]{:S(2)}, u32[]{:S(2)}) %all-to-all-start.2) | async-done | bytes 524320 | tf_op jit(solution)/shard_map/all_to_all | solution.py:32
  (74 shorter events, 69.6 us)
Async XLA Ops:
  20.0 16.2 %all-to-all-start = ((bf16[16,2,32,128]{3,2,1,0:T(8,128)(2,1)}), bf16[16,2,32,128]{3,2,1,0:T(8,128)(2,1)S(1)}, u32[]{:S(2)}, u32[]{:S(2)}) async-start(bf16[16,2,32,128]{3,2,1,0:T(8,128)(2,1)} %broadcast_in_dim.13), calls=%async_computation | async-start | bytes 524288 | tf_op jit(solution)/shard_map/all_to_all | solution.py:17
  28.4 13.5 %copy-start.1 = (bf16[1024,128]{1,0:T(8,128)(2,1)S(1)}, bf16[1024,128]{1,0:T(8,128)(2,1)}, u32[]{:S(2)}) copy-start(bf16[1024,128]{1,0:T(8,128)(2,1)} %param.9) | copy-start | bytes 786436
  28.4 13.5 %copy-start.2 = (f32[128]{0:T(128)S(1)}, f32[128]{0:T(128)}, u32[]{:S(2)}) copy-start(f32[128]{0:T(128)} %param.10) | copy-start | bytes 1540
  61.4 1.9 copy-start
  88.9 1.9 copy-start
  116.4 1.9 copy-start
  143.9 1.9 copy-start
  171.4 1.9 copy-start
  198.9 1.9 copy-start
  226.4 1.9 copy-start
  253.9 1.9 copy-start
  263.0 17.9 %all-to-all-start.3 = ((f32[16,2,32,128]{3,1,2,0:T(2,128)}), f32[16,2,32,128]{3,1,2,0:T(2,128)S(1)}, u32[]{:S(2)}, u32[]{:S(2)}) async-start(f32[16,2,32,128]{3,1,2,0:T(2,128)} %copy.37), calls=%async_computation.3 | async-start | bytes 1048576 | tf_op jit(solution)/shard_map/all_to_all | solution.py:32
  280.8 17.3 %all-to-all-start.2 = ((f32[16,2,32,128]{3,2,1,0:T(8,128)}), f32[16,2,32,128]{3,2,1,0:T(8,128)S(1)}, u32[]{:S(2)}, u32[]{:S(2)}) async-start(f32[16,2,32,128]{3,2,1,0:T(8,128)} %bitcast.2), calls=%async_computation.2 | async-start | bytes 1048576 | tf_op jit(solution)/shard_map/all_to_all | solution.py:32
where the time goes:
time: 303 us; the launch traced here: 299 us
  local copies, waits for them, and re-layouts  132 us (44%)
  matrix products  99.1 us (33%)
  waiting for transfers between devices  29.8 us (10%)
  starting transfers between devices  19.2 us (6%)
  blocking collectives  16.9 us (6%)
    convert_element_type x8, local copies, waits for them, and re-layouts, block_step(): d_outer.astype(jnp.bfloat16)  52.2 us
    while x24, local copies, waits for them, and re-layouts  44.1 us
    dot_general x8, matrix products, block_step(): jnp.einsum('ijce,sci->sej', d_outer, left_block, preferred_element_type=j...  38.4 us
    dot_general x8, matrix products, block_step(): lax.dot_general(cot_flat, out_weight, (((1,), (1,)), ((), ())), preferred...  25.5 us
    all_to_all x2, waiting for transfers between devices, summed_on_arrival(): lax.all_to_all(blocks, axis, split_axis=0, concat_axis=0, tiled=True)  22 us
    all_to_all x1, blocking collectives, copy_for_each(): return lax.all_to_all(copies, axis, split_axis=0, concat_axis=0, tiled=True)  16.9 us
    dot_general x8, matrix products, block_step(): jnp.dot(outer_flat, out_weight, preferred_element_type=jnp.float32)  15.7 us
    dynamic_update_slice x8, local copies, waits for them, and re-layouts, block_step(): pairs = lax.dynamic_update_slice_in_dim(pairs, pair_out, start, 0)  15.3 us
  transfers between devices with their start and end apart: 3, of which 3 were waited for; matrix products, arithmetic and copies ran while one was open for 1% of the time, Pallas kernels for 0%

commit v1 on v0

v1 whole, which is shorter than its diff:
```python
import functools

import jax
import jax.numpy as jnp
from jax import lax
from jax.experimental import pallas as pl
from jax.experimental.pallas import tpu as pltpu
from jax.sharding import PartitionSpec as P

F32 = jnp.float32
BF16 = jnp.bfloat16
MESH = pl.DeviceIdType.MESH

N = 16
S = 32
C = 32
K = 128
T = 128
H = S // 2
IC = 16
IB = 8
NEAR = ((0, 1), (1, 0), (1, 1), (3, 0), (3, 1), (2, 0), (2, 1))
ALL_YC = ((0, 0), (0, 1), (1, 0), (1, 1), (3, 0), (3, 1), (2, 0), (2, 1))


def owner(h, half):
    return 4 * (h // 2) + 2 * half + h % 2


def greet(barrier, me_w, me_n):
    for d in range(1, N):
        pl.semaphore_signal(
            barrier, inc=1, device_id={"wide": (me_w + d) % N}, device_id_type=MESH
        )
        pl.semaphore_signal(
            barrier, inc=1, device_id={"narrow": (me_n + d) % N}, device_id_type=MESH
        )


def cot_copies(cot_hbm, cot_buf, sems):
    return [
        pltpu.make_async_copy(
            cot_hbm.at[pl.ds(t * IC, IC)], cot_buf.at[pl.ds(t * IC, IC)], sems.at[t]
        )
        for t in range(T // IC)
    ]


def left_gradient_half(rows_ref, w2t_ref, cot_hbm, cot_buf, cot_sem, spread, sums):
    def step(t, _):
        base = pl.multiple_of(t * IC, IC)
        pltpu.make_async_copy(
            cot_hbm.at[pl.ds(base, IC)], cot_buf.at[pl.ds(base, IC)], cot_sem.at[t]
        ).wait()
        for p in range(IC // 2):
            pair = jnp.concatenate([cot_buf[base + 2 * p], cot_buf[base + 2 * p + 1]], axis=1)
            g = jnp.dot(rows_ref[...], pair, preferred_element_type=F32).astype(BF16)
            for q in range(2):
                r = (2 * p + q) * H
                for e in range(C):
                    spread[r : r + H, e * K : (e + 1) * K] = g[
                        e * H : (e + 1) * H, q * K : (q + 1) * K
                    ]
        out = jnp.dot(spread[...], w2t_ref[...], preferred_element_type=F32)
        sums[pl.ds(pl.multiple_of(t * IC * H, IC * H), IC * H), 0:C] = out * (1.0 / S)
        return 0

    lax.fori_loop(0, T // IC, step, 0)


def blocks_of(sums, blocks):
    for s in range(H):
        mine = sums[pl.ds(s, T, stride=H), :]
        blocks[s // 2, (s % 2) * C : (s % 2 + 1) * C, :] = mine.T[0:C, :].astype(BF16)


def gather_kernel(
    left_ref, right_ref, w_ref, cot_hbm,
    lt_ref, rt_ref, rb_ref, w2_ref, w2t_ref, first_ref,
    l_buf, r_buf, cot_buf, wide_f, rows_a, lt_f, spread, sums,
    cot_sem, lsend, lrecv, rsend, rrecv,
):
    me_w = lax.axis_index("wide")
    me_n = lax.axis_index("narrow")
    x_hi = (me_w // 2) % 2
    y = me_w // 4
    core = me_w % 2
    barrier = pltpu.get_barrier_semaphore()
    greet(barrier, me_w, me_n)
    for copy in cot_copies(cot_hbm, cot_buf, cot_sem):
        copy.start()

    wide_f[...] = w_ref[...].astype(F32)
    for e in range(C):
        part = wide_f[pl.ds(e, C, stride=C), :]
        w2_ref[:, e * K : (e + 1) * K] = part.astype(BF16)
        w2t_ref[e * K : (e + 1) * K, :] = part.T.astype(BF16)

    pl.semaphore_wait(barrier, 2 * (N - 1))

    def right_copy(dy, dx, dc):
        to = ((y + dy) % 4) * 4 + ((x_hi + dx) % 2) * 2 + (core + dc) % 2
        k = dy * 4 + dx * 2 + dc
        return pltpu.make_async_remote_copy(
            right_ref, r_buf.at[me_w], rsend.at[k], rrecv.at[me_w],
            device_id={"wide": to}, device_id_type=MESH,
        )

    def left_copy(d):
        return pltpu.make_async_remote_copy(
            left_ref, l_buf.at[me_n], lsend.at[d], lrecv.at[me_n],
            device_id={"narrow": (me_n + d) % N}, device_id_type=MESH,
        )

    sends = [right_copy(dy, 0, dc) for dy, dc in NEAR]
    sends += [left_copy(d) for d in (1, 15, 8, 2, 14, 9, 7, 3, 13, 10, 6, 4, 12, 11, 5)]
    sends += [right_copy(dy, 1, dc) for dy, dc in ALL_YC]
    for copy in sends:
        copy.start()
    r_buf[me_w] = right_ref[...]
    l_buf[me_n] = left_ref[...]

    def right_arrived(w):
        pltpu.make_async_remote_copy(
            right_ref, r_buf.at[w], rsend.at[0], rrecv.at[w],
            device_id={"wide": w}, device_id_type=MESH,
        ).wait_recv()

    def left_arrived(n):
        pltpu.make_async_remote_copy(
            left_ref, l_buf.at[n], lsend.at[0], lrecv.at[n],
            device_id={"narrow": n}, device_id_type=MESH,
        ).wait_recv()

    for dy, dc in NEAR:
        right_arrived(((y + dy) % 4) * 4 + x_hi * 2 + (core + dc) % 2)
    for h in range(8):
        wide_f[h * 64 : (h + 1) * 64, :] = r_buf[owner(h, x_hi)].astype(F32)
    for e in range(C):
        rows_a[e * H : (e + 1) * H, :] = wide_f[pl.ds(e, H, stride=C), :].astype(BF16)

    left_gradient_half(rows_a, w2t_ref, cot_hbm, cot_buf, cot_sem, spread, sums)
    blocks_of(sums, first_ref)

    for dy, dc in ALL_YC:
        right_arrived(((y + dy) % 4) * 4 + (1 - x_hi) * 2 + (core + dc) % 2)
    for h in range(8):
        wide_f[h * 64 : (h + 1) * 64, :] = r_buf[owner(h, 1 - x_hi)].astype(F32)
    for e in range(C):
        rb_ref[e * H : (e + 1) * H, :] = wide_f[pl.ds(e, H, stride=C), :].astype(BF16)
    for w in range(N):
        wide_f[w * 64 : (w + 1) * 64, :] = r_buf[w].astype(F32)
    for b in range(8):
        rows = jnp.concatenate(
            [wide_f[pl.ds(4 * b + q, S, stride=C), :] for q in range(4)], axis=0
        )
        rt_ref[:, b * 128 : (b + 1) * 128] = rows.T.astype(BF16)
    for d in range(1, N):
        left_arrived((me_n + d) % N)
    for n in range(N):
        for q in range(2):
            part = l_buf[n, q * C : (q + 1) * C, :].astype(F32) * (1.0 / S)
            lt_f[pl.ds(2 * n + q, T, stride=S), 0:C] = part.T
    lt_ref[...] = lt_f[:, 0:C].astype(BF16)
    for copy in sends:
        copy.wait_send()


def gather(left, right, weight, cot):
    vmem = pl.BlockSpec(memory_space=pltpu.VMEM)
    return pl.pallas_call(
        gather_kernel,
        out_shape=(
            jax.ShapeDtypeStruct((T * S, C), BF16),
            jax.ShapeDtypeStruct((T, C * S), BF16),
            jax.ShapeDtypeStruct((C * H, T), BF16),
            jax.ShapeDtypeStruct((C, C * K), BF16),
            jax.ShapeDtypeStruct((C * K, C), BF16),
            jax.ShapeDtypeStruct((8, 64, T), BF16),
        ),
        in_specs=[vmem, vmem, vmem, pl.BlockSpec(memory_space=pl.ANY)],
        out_specs=(vmem,) * 6,
        scratch_shapes=[
            pltpu.VMEM((N, 64, T), BF16),
            pltpu.VMEM((N, 64, T), BF16),
            pltpu.VMEM((T, T, K), BF16),
            pltpu.VMEM((C * S, 128), F32),
            pltpu.VMEM((C * H, T), BF16),
            pltpu.VMEM((T * S, 128), F32),
            pltpu.VMEM((IC * H, C * K), BF16),
            pltpu.VMEM((T * H, 128), F32),
            pltpu.SemaphoreType.DMA((T // IC,)),
            pltpu.SemaphoreType.DMA((N,)),
            pltpu.SemaphoreType.DMA((N,)),
            pltpu.SemaphoreType.DMA((N,)),
            pltpu.SemaphoreType.DMA((N,)),
        ],
        compiler_params=pltpu.CompilerParams(
            collective_id=0, has_side_effects=True, vmem_limit_bytes=48 << 20
        ),
        name="gather_kernel",
    )(left, right, weight, cot)


def pair_kernel(lt_ref, rt_ref, w2_ref, bias_ref, cot_ref, pair_ref, dr_ref, t_buf, acc):
    g = pl.program_id(0)

    @pl.when(g == 0)
    def _():
        acc[...] = jnp.zeros_like(acc)

    lt = lt_ref[...]
    for b in range(C // 2):
        t = jnp.dot(lt, w2_ref[:, b * 256 : (b + 1) * 256], preferred_element_type=F32)
        t = t.astype(BF16)
        for i in range(IB):
            for q in range(2):
                e = 2 * b + q
                t_buf[e * S : (e + 1) * S, i * K : (i + 1) * K] = t[
                    i * S : (i + 1) * S, q * K : (q + 1) * K
                ]
    out = jnp.dot(rt_ref[...], t_buf[...], preferred_element_type=F32)
    for i in range(IB):
        pair_ref[i] = (out[:, i * K : (i + 1) * K] + bias_ref[...]).astype(BF16)
    cot = jnp.concatenate([cot_ref[i] for i in range(IB)], axis=1)
    acc[...] += lax.dot_general(
        t_buf[...], cot, (((1,), (1,)), ((), ())), preferred_element_type=F32
    )

    @pl.when(g == pl.num_programs(0) - 1)
    def _():
        for s in range(S):
            dr_ref[s // 2, (s % 2) * C : (s % 2 + 1) * C, :] = acc[
                pl.ds(s, C, stride=S), :
            ].astype(BF16)


def pairs(lt, rt, w2, bias, cot):
    whole = lambda shape: pl.BlockSpec(shape, lambda g: (0,) * len(shape))
    return pl.pallas_call(
        pair_kernel,
        grid=(T // IB,),
        out_shape=(
            jax.ShapeDtypeStruct((T, T, K), BF16),
            jax.ShapeDtypeStruct((N, 64, T), BF16),
        ),
        in_specs=[
            pl.BlockSpec((IB * S, C), lambda g: (g, 0)),
            whole((T, C * S)),
            whole((C, C * K)),
            whole((1, K)),
            pl.BlockSpec((IB, T, K), lambda g: (g, 0, 0)),
        ],
        out_specs=(pl.BlockSpec((IB, T, K), lambda g: (g, 0, 0)), whole((N, 64, T))),
        scratch_shapes=[pltpu.VMEM((C * S, IB * K), BF16), pltpu.VMEM((C * S, T), F32)],
        compiler_params=pltpu.CompilerParams(
            dimension_semantics=("arbitrary",), vmem_limit_bytes=48 << 20
        ),
        name="pair_kernel",
    )(lt, rt, w2, bias, cot)


def scatter_kernel(
    dr_ref, first_ref, rb_ref, w2t_ref, cot_hbm,
    gl_ref, gr_ref,
    dr_in, dl_in, second, cot_buf, spread, sums,
    cot_sem, rsend, rrecv, lsend, lrecv,
):
    me_w = lax.axis_index("wide")
    me_n = lax.axis_index("narrow")
    x_hi = (me_w // 2) % 2
    barrier = pltpu.get_barrier_semaphore()
    greet(barrier, me_w, me_n)
    for copy in cot_copies(cot_hbm, cot_buf, cot_sem):
        copy.start()
    pl.semaphore_wait(barrier, 2 * (N - 1))

    def right_copy(d):
        to = (me_w + d) % N
        return pltpu.make_async_remote_copy(
            dr_ref.at[to], dr_in.at[me_w], rsend.at[d], rrecv.at[me_w],
            device_id={"wide": to}, device_id_type=MESH,
        )

    def left_copy(blocks, h, half):
        to = owner(h, half)
        return pltpu.make_async_remote_copy(
            blocks.at[h], dl_in.at[me_n], lsend.at[to], lrecv.at[me_n],
            device_id={"narrow": to}, device_id_type=MESH,
        )

    for d in range(1, N):
        right_copy(d).start()
    for h in range(8):
        @pl.when(owner(h, x_hi) != me_n)
        def _():
            left_copy(first_ref, h, x_hi).start()

    left_gradient_half(rb_ref, w2t_ref, cot_hbm, cot_buf, cot_sem, spread, sums)
    blocks_of(sums, second)
    for h in range(8):
        @pl.when(owner(h, 1 - x_hi) != me_n)
        def _():
            left_copy(second, h, 1 - x_hi).start()

    for h in range(8):
        @pl.when(owner(h, x_hi) == me_n)
        def _():
            dl_in[me_n] = first_ref[h]

        @pl.when(owner(h, 1 - x_hi) == me_n)
        def _():
            dl_in[me_n] = second[h]

    dr_in[me_w] = dr_ref[me_w]
    for d in range(1, N):
        w = (me_w + d) % N
        pltpu.make_async_remote_copy(
            dr_ref.at[w], dr_in.at[w], rsend.at[d], rrecv.at[w],
            device_id={"wide": w}, device_id_type=MESH,
        ).wait_recv()
    total = dr_in[0].astype(F32)
    for w in range(1, N):
        total += dr_in[w].astype(F32)
    gr_ref[...] = total
    for d in range(1, N):
        n = (me_n + d) % N
        pltpu.make_async_remote_copy(
            second.at[0], dl_in.at[n], lsend.at[n], lrecv.at[n],
            device_id={"narrow": n}, device_id_type=MESH,
        ).wait_recv()
    total = dl_in[0].astype(F32)
    for n in range(1, N):
        total += dl_in[n].astype(F32)
    gl_ref[...] = total
    for d in range(1, N):
        right_copy(d).wait_send()
    for h in range(8):
        @pl.when(owner(h, x_hi) != me_n)
        def _():
            left_copy(first_ref, h, x_hi).wait_send()

        @pl.when(owner(h, 1 - x_hi) != me_n)
        def _():
            left_copy(second, h, 1 - x_hi).wait_send()


def scatter(dr, first, rb, w2t, cot):
    vmem = pl.BlockSpec(memory_space=pltpu.VMEM)
    return pl.pallas_call(
        scatter_kernel,
        out_shape=(
            jax.ShapeDtypeStruct((64, T), F32),
            jax.ShapeDtypeStruct((64, T), F32),
        ),
        in_specs=[vmem] * 4 + [pl.BlockSpec(memory_space=pl.ANY)],
        out_specs=(vmem, vmem),
        scratch_shapes=[
            pltpu.VMEM((N, 64, T), BF16),
            pltpu.VMEM((N, 64, T), BF16),
            pltpu.VMEM((8, 64, T), BF16),
            pltpu.VMEM((T, T, K), BF16),
            pltpu.VMEM((IC * H, C * K), BF16),
            pltpu.VMEM((T * H, 128), F32),
            pltpu.SemaphoreType.DMA((T // IC,)),
            pltpu.SemaphoreType.DMA((N,)),
            pltpu.SemaphoreType.DMA((N,)),
            pltpu.SemaphoreType.DMA((N,)),
            pltpu.SemaphoreType.DMA((N,)),
        ],
        compiler_params=pltpu.CompilerParams(
            collective_id=1, has_side_effects=True, vmem_limit_bytes=48 << 20
        ),
        name="scatter_kernel",
    )(dr, first, rb, w2t, cot)


def local(left, right, out_weight, out_bias, cotangent):
    lt, rt, rb, w2, w2t, first = gather(
        left.reshape(64, T), right.reshape(64, T), out_weight, cotangent
    )
    pair_update, dr = pairs(lt, rt, w2, out_bias.reshape(1, K), cotangent)
    gl, gr = scatter(dr, first, rb, w2t, cotangent)
    return pair_update, gl.reshape(2, C, T), gr.reshape(2, C, T)


def solution(mesh):
    return jax.shard_map(
        local,
        mesh=mesh,
        in_specs=(
            P("narrow", None, "wide"),
            P("wide", None, "narrow"),
            P(),
            P(),
            P("wide", "narrow", None),
        ),
        out_specs=(P("wide", "narrow", None), P("narrow", None, "wide"), P("wide", None, "narrow")),
        check_vma=False,
    )
```

time: 303 us -> 79.4 us (0.26)
  local copies, waits for them, and re-layouts: 132 us -> 4 us
  matrix products: 99.1 us -> 0 us
  Pallas kernels: 0 us -> 73.3 us
  waiting for transfers between devices: 29.8 us -> 0 us
  starting transfers between devices: 19.2 us -> 0 us
  blocking collectives: 16.9 us -> 0 us
    dot_general x40 -> x0, matrix products: 99.1 us -> none  [the longest x8 38.4 us: block_step(): jnp.einsum('ijce,sci->sej', d_outer, left_block, preferred_element_type=j...]
    pallas_call x0 -> x3, Pallas kernels: none -> 73.3 us  [the longest x1 28.1 us: gather(): pl.pallas_call(gather_kernel, out_shape=(jax.ShapeDtypeStruct((T * S, C),...]
    convert_element_type x8 -> x0, local copies, waits for them, and re-layouts: 52.2 us -> none  [block_step(): d_outer.astype(jnp.bfloat16)]
    while x25 -> x0, local copies, waits for them, and re-layouts: 45.5 us -> none
    all_to_all x3 -> x0, waiting for transfers between devices: 29.8 us -> none  [the longest x2 22 us: summed_on_arrival(): lax.all_to_all(blocks, axis, split_axis=0, concat_axis=0, tiled=True)]
    all_to_all x3 -> x0, starting transfers between devices: 19.2 us -> none  [the longest x2 10.9 us: summed_on_arrival(): lax.all_to_all(blocks, axis, split_axis=0, concat_axis=0, tiled=True)]
    all_to_all x1 -> x0, blocking collectives: 16.9 us -> none  [copy_for_each(): return lax.all_to_all(copies, axis, split_axis=0, concat_axis=0, tiled=True)]
    dynamic_update_slice x8 -> x0, local copies, waits for them, and re-layouts: 15.3 us -> none  [block_step(): pairs = lax.dynamic_update_slice_in_dim(pairs, pair_out, start, 0)]
  transfers between devices with their start and end apart: 3 -> 0, of which waited for: 3 -> 0; matrix products, arithmetic and copies ran while one was open for 1% -> 0% of each run, Pallas kernels for 0% -> 0%
where the time goes in v1:
time: 79.4 us; the launch traced here: 78 us
  Pallas kernels  73.3 us (92%)
  local copies, waits for them, and re-layouts  4 us (5%)
    pallas_call x1, Pallas kernels, gather(): pl.pallas_call(gather_kernel, out_shape=(jax.ShapeDtypeStruct((T * S, C),...  28.1 us
    pallas_call x1, Pallas kernels, pairs(): pl.pallas_call(pair_kernel, grid=(T // IB,), out_shape=(jax.ShapeDtypeStr...  26.4 us
    pallas_call x1, Pallas kernels, scatter(): pl.pallas_call(scatter_kernel, out_shape=(jax.ShapeDtypeStruct((64, T), F...  18.8 us
    unnamed x12, local copies, waits for them, and re-layouts  4 us

profile of v1, /device:TPU:1, one launch (start us, length us, event | category | flops | bytes accessed | tf_op | source)
XLA Modules:
  0.0 78.0 jit_solution(9122584517555769183)
XLA Ops:
  0.6 0.0 copy-start
  0.6 0.0 copy-start.1
  0.7 1.1 %copy-done.1 = bf16[1024,128]{1,0:T(8,128)(2,1)S(1)} copy-done((bf16[1024,128]{1,0:T(8,128)(2,1)S(1)}, bf16[1024,128]{1,0:T(8,128)(2,1)}, u32[]{:S(2)}) %copy-start.1) | copy-done | bytes 262168
  1.7 0.0 copy-start.2
  1.7 0.9 %copy-done.2 = bf16[2,32,128]{2,1,0:T(8,128)(2,1)S(1)} copy-done((bf16[2,32,128]{2,1,0:T(8,128)(2,1)S(1)}, bf16[2,32,128]{2,1,0:T(8,128)(2,1)}, u32[]{:S(2)}) %copy-start.2) | copy-done | bytes 16408
  2.7 0.0 copy-start.3
  2.7 0.7 copy-done.3
  3.4 0.0 copy-start.4
  3.4 28.1 %gather_kernel.1 = (bf16[4096,32]{1,0:T(8,128)(2,1)S(1)}, bf16[128,1024]{1,0:T(8,128)(2,1)S(1)}, bf16[512,128]{1,0:T(8,128)(2,1)S(1)}, bf16[32,4096]{1,0:T(8,128...) custom-call(bf16[64,128]{1,0:T(8,128)(2,1)S(1)} %bitcast.7, bf16[64,128]{1,0:T(8,128)(2,1)S(1)} %bitcast.8, ...), custom_call_target="tpu_custom_call" | custom-call | tf_op jit(solution)/shard_map/gather_kernel/pallas_call | solution.py:171
  31.5 0.0 copy-done
  31.6 0.0 copy-done.4
  31.6 26.4 %pair_kernel.1 = (bf16[128,128,128]{2,1,0:T(8,128)(2,1)}, bf16[16,64,128]{2,1,0:T(8,128)(2,1)S(1)}) custom-call(bf16[4096,32]{1,0:T(8,128)(2,1)S(1)} %get-tuple-element.13.lt_ref, bf16[128,1024]{1,0:T(8,128)(2,1)S(1)} %get-tuple-element.14.rt_ref, bf16[32,4096]{1,0:T(8,128)(2,1)S(1)} %get-tuple-element.15.w2_ref, f32[1,128]{1,0:T(1,128)S(1)} %bitcast.9, ...), custom_call_target="tpu_custom_call" | custom-call | tf_op jit(solution)/shard_map/pair_kernel/pallas_call | solution.py:240
  57.9 18.8 %scatter_kernel.1 = (f32[64,128]{1,0:T(8,128)S(1)}, f32[64,128]{1,0:T(8,128)S(1)}) custom-call(bf16[16,64,128]{2,1,0:T(8,128)(2,1)S(1)} %get-tuple-element.17.dr_ref, bf16[8,64,128]{2,1,0:T(8,128)(2,1)S(1)} %get-tuple-element.18.first_ref, bf16[512,128]{1,0:T(8,128)(2,1)S(1)} %get-tuple-element.19.rb_ref, bf16[4096,32]{1,0:T(8,128)(2,1)S(1)} %get-tuple-element.20.w2t_ref, ...), custom_call_target="tpu_custom_call" | custom-call | tf_op jit(solution)/shard_map/scatter_kernel/pallas_call | solution.py:350
  76.8 0.6 copy.10
  77.4 0.6 copy.11
Async XLA Ops:
  0.6 30.9 %copy-start = (bf16[128,128,128]{2,1,0:T(8,128)(2,1)S(1)}, bf16[128,128,128]{2,1,0:T(8,128)(2,1)}, u32[]{:S(2)}) copy-start(bf16[128,128,128]{2,1,0:T(8,128)(2,1)} %cot_hbm.3) | copy-start | bytes 12582916
  0.6 1.1 %copy-start.1 = (bf16[1024,128]{1,0:T(8,128)(2,1)S(1)}, bf16[1024,128]{1,0:T(8,128)(2,1)}, u32[]{:S(2)}) copy-start(bf16[1024,128]{1,0:T(8,128)(2,1)} %w_ref.1) | copy-start | bytes 786436
  1.7 0.9 %copy-start.2 = (bf16[2,32,128]{2,1,0:T(8,128)(2,1)S(1)}, bf16[2,32,128]{2,1,0:T(8,128)(2,1)}, u32[]{:S(2)}) copy-start(bf16[2,32,128]{2,1,0:T(8,128)(2,1)} %param.5) | copy-start | bytes 49156
  2.7 0.7 copy-start.3
  3.4 28.1 %copy-start.4 = (f32[128]{0:T(128)S(1)}, f32[128]{0:T(128)}, u32[]{:S(2)}) copy-start(f32[128]{0:T(128)} %param.8) | copy-start | bytes 1540

commit v2 on v0

v2 whole, which is shorter than its diff:
```python
import jax
import jax.numpy as jnp
from jax import lax
from jax.experimental import pallas as pl
from jax.experimental.pallas import tpu as pltpu
from jax.sharding import PartitionSpec as P

F32 = jnp.float32
BF16 = jnp.bfloat16
MESH = pl.DeviceIdType.MESH
NT = (((1,), (1,)), ((), ()))

N = 16
S = 32
C = 32
K = 128
T = 128
HALF = T // 2
IC = 16
IM = 16
IB = 8
NEAR_FIRST = (1, 15, 8, 2, 14, 9, 7, 3, 13, 10, 6, 4, 12, 11, 5)


def greet(barrier, me_w, me_n):
    for d in range(1, N):
        pl.semaphore_signal(
            barrier, inc=1, device_id={"wide": (me_w + d) % N}, device_id_type=MESH
        )
        pl.semaphore_signal(
            barrier, inc=1, device_id={"narrow": (me_n + d) % N}, device_id_type=MESH
        )


def push(axis, me, d, src, dst, send_sem, recv_sem):
    return pltpu.make_async_remote_copy(
        src, dst.at[me], send_sem.at[d], recv_sem.at[me],
        device_id={axis: (me + d) % N}, device_id_type=MESH,
    )


def arrived(axis, me, d, src, dst, send_sem, recv_sem):
    peer = (me + d) % N
    pltpu.make_async_remote_copy(
        src, dst.at[peer], send_sem.at[d], recv_sem.at[peer],
        device_id={axis: peer}, device_id_type=MESH,
    ).wait_recv()


def cot_copy(cot_hbm, cot_buf, sems, first, t):
    at = pl.multiple_of(t * IC, IC)
    return pltpu.make_async_copy(
        cot_hbm.at[pl.ds(first + at, IC)], cot_buf.at[pl.ds(at, IC)], sems.at[t]
    )


def project_cotangent(first, steps, wec_ref, cot_hbm, cot_buf, cot_sem, spread):
    def step(t, _):
        cot_copy(cot_hbm, cot_buf, cot_sem, first, t).wait()
        base = t * IC
        for p in range(IC // 2):
            rows = cot_buf[pl.ds(base + 2 * p, 2)].reshape(2 * T, K)
            d = lax.dot_general(wec_ref[...], rows, NT, preferred_element_type=F32)
            d = d.astype(BF16)
            for q in range(2):
                for e in range(C):
                    spread[base + 2 * p + q, e] = d[e * C : (e + 1) * C, q * T : (q + 1) * T]
        return 0

    lax.fori_loop(steps[0], steps[1], step, 0)


def left_gradient(spread, rmat_ref, sums, beside):
    def step(t, _):
        at = pl.multiple_of(t * IM * C, IM * C)
        rows = jnp.concatenate(
            [spread[pl.ds(t * IM, IM), e].reshape(IM * C, T) for e in range(C)], axis=1
        )
        out = jnp.dot(rows, rmat_ref[...], preferred_element_type=F32)
        sums[pl.ds(at, IM * C), 0:S] = out * (1.0 / S)
        beside(t)
        return 0

    lax.fori_loop(0, HALF // IM, step, 0)


def blocks_of(sums, turned, blocks):
    for c in range(C):
        part = sums[pl.ds(c, HALF, stride=C), :].T
        turned[c * N : (c + 1) * N, :] = jnp.concatenate([part[0:N], part[N : 2 * N]], axis=1)
    for n in range(N):
        blocks[n] = turned[pl.ds(n, C, stride=N), :].astype(BF16)


def gather_kernel(
    left_hbm, right_hbm, w_hbm, cot_hbm,
    lt_ref, rt_ref, w2_ref, wec_ref, rmat_ref, first_ref,
    left_v, right_v, w_v, l_buf, r_buf, cot_buf, wide_f, left_f, lt_f, spread, sums, turned,
    in_sem, cot_sem, lsend, lrecv, rsend, rrecv,
):
    me_w = lax.axis_index("wide")
    me_n = lax.axis_index("narrow")
    barrier = pltpu.get_barrier_semaphore()
    fetch_w = pltpu.make_async_copy(w_hbm, w_v, in_sem.at[0])
    fetch_l = pltpu.make_async_copy(left_hbm, left_v, in_sem.at[1])
    fetch_r = pltpu.make_async_copy(right_hbm, right_v, in_sem.at[2])
    fetch_w.start()
    fetch_l.start()
    fetch_r.start()
    for t in range(HALF // IC):
        cot_copy(cot_hbm, cot_buf, cot_sem, 0, t).start()
    greet(barrier, me_w, me_n)

    fetch_w.wait()
    wide_f[...] = w_v[...].astype(F32)
    for e in range(C):
        part = wide_f[pl.ds(e, C, stride=C), :].astype(BF16)
        w2_ref[e] = part
        wec_ref[e * C : (e + 1) * C, :] = part
    fetch_l.wait()
    fetch_r.wait()

    project_cotangent(0, (0, AHEAD), wec_ref, cot_hbm, cot_buf, cot_sem, spread)
    pl.semaphore_wait(barrier, 2 * (N - 1))
    sends = [
        push("wide", me_w, d, right_v, r_buf, rsend, rrecv) for d in NEAR_FIRST
    ]
    sends += [
        push("narrow", me_n, d, left_v, l_buf, lsend, lrecv) for d in NEAR_FIRST
    ]
    for copy in sends:
        copy.start()
    project_cotangent(0, (AHEAD, HALF // IC), wec_ref, cot_hbm, cot_buf, cot_sem, spread)

    r_buf[me_w] = right_v[...]
    l_buf[me_n] = left_v[...]
    for d in range(1, N):
        arrived("wide", me_w, d, right_v, r_buf, rsend, rrecv)
    for w in range(N):
        wide_f[w * 64 : (w + 1) * 64, :] = r_buf[w].astype(F32)
    for e in range(C):
        rows = jnp.concatenate(
            [wide_f[pl.ds(q * C + e, N, stride=2 * C), :] for q in range(2)], axis=0
        )
        rmat_ref[e * T : (e + 1) * T, :] = rows.T.astype(BF16)
    for d in range(1, N):
        arrived("narrow", me_n, d, left_v, l_buf, lsend, lrecv)
    for n in range(N):
        left_f[n * 64 : (n + 1) * 64, :] = l_buf[n].astype(F32) * (1.0 / S)

    def beside(t):
        for b in range(2):
            rows = jnp.concatenate(
                [wide_f[pl.ds(8 * t + 4 * b + q, S, stride=C), :] for q in range(4)], axis=0
            )
            rt_ref[2 * t + b] = rows.T.astype(BF16)
        for q in range(8):
            s = 8 * t + q
            part = left_f[pl.ds(pl.multiple_of(s * C, C), C), :]
            lt_f[pl.ds(s, T, stride=S), 0:C] = part.T

    left_gradient(spread, rmat_ref, sums, beside)
    lt_ref[...] = lt_f[:, 0:C].astype(BF16)
    blocks_of(sums, turned, first_ref)
    for copy in sends:
        copy.wait_send()


def gather(left, right, weight, cot):
    vmem = pl.BlockSpec(memory_space=pltpu.VMEM)
    hbm = pl.BlockSpec(memory_space=pltpu.HBM)
    return pl.pallas_call(
        gather_kernel,
        out_shape=(
            jax.ShapeDtypeStruct((T * S, C), BF16),
            jax.ShapeDtypeStruct((C // 4, T, 4 * S), BF16),
            jax.ShapeDtypeStruct((C, C, K), BF16),
            jax.ShapeDtypeStruct((C * C, K), BF16),
            jax.ShapeDtypeStruct((C * T, S), BF16),
            jax.ShapeDtypeStruct((N, C, T), BF16),
        ),
        in_specs=[hbm] * 4,
        out_specs=(vmem,) * 6,
        scratch_shapes=[
            pltpu.VMEM((64, T), BF16),
            pltpu.VMEM((64, T), BF16),
            pltpu.VMEM((C * C, K), BF16),
            pltpu.VMEM((N, 64, T), BF16),
            pltpu.VMEM((N, 64, T), BF16),
            pltpu.VMEM((HALF, T, K), BF16),
            pltpu.VMEM((C * S, 128), F32),
            pltpu.VMEM((C * S, 128), F32),
            pltpu.VMEM((T * S, 128), F32),
            pltpu.VMEM((HALF, C, C, T), BF16),
            pltpu.VMEM((HALF * C, 128), F32),
            pltpu.VMEM((C * N, 128), F32),
            pltpu.SemaphoreType.DMA((3,)),
            pltpu.SemaphoreType.DMA((HALF // IC,)),
            pltpu.SemaphoreType.DMA((N,)),
            pltpu.SemaphoreType.DMA((N,)),
            pltpu.SemaphoreType.DMA((N,)),
            pltpu.SemaphoreType.DMA((N,)),
        ],
        compiler_params=pltpu.CompilerParams(
            collective_id=0, has_side_effects=True, vmem_limit_bytes=40 << 20
        ),
        name="gather_kernel",
    )(*[pltpu.with_memory_space_constraint(x, pltpu.HBM) for x in (left, right, weight, cot)])


AHEAD = 2


def intermediate_tile(lt, w2_ref, t_buf, b):
    w = jnp.concatenate([w2_ref[2 * b], w2_ref[2 * b + 1]], axis=1)
    t = jnp.dot(lt, w, preferred_element_type=F32).astype(BF16)
    for i in range(IB):
        for q in range(2):
            e = 2 * b + q
            t_buf[i, e * S : (e + 1) * S, :] = t[i * S : (i + 1) * S, q * K : (q + 1) * K]


def pair_kernel(lt_ref, rt_ref, w2_ref, bias_ref, cot_ref, pair_ref, dr_ref, t_a, t_b, acc_t, acc):
    g = pl.program_id(0)

    def lt_of(chunk):
        at = jnp.minimum(chunk, T // IB - 1) * (IB * S)
        return lt_ref[pl.ds(pl.multiple_of(at, IB * S), IB * S), :]

    @pl.when(g == 0)
    def _():
        acc_t[...] = jnp.zeros_like(acc_t)
        lt = lt_of(0)
        for b in range(C // 2):
            intermediate_tile(lt, w2_ref, t_a, b)

    for half, (now, later) in enumerate(((t_a, t_b), (t_b, t_a))):
        lt = lt_of(2 * g + half + 1)
        first = half * IB
        cot = jnp.concatenate([cot_ref[first + i] for i in range(IB)], axis=1)

        def pair_of(p):
            rows = jnp.concatenate([rt_ref[b] for b in range(C // 4)], axis=1)
            both = jnp.concatenate([now[2 * p], now[2 * p + 1]], axis=1)
            out = jnp.dot(rows, both, preferred_element_type=F32)
            for q in range(2):
                pair_ref[first + 2 * p + q] = (
                    out[:, q * K : (q + 1) * K] + bias_ref[...]
                ).astype(BF16)

        def right_of(n):
            turned = jnp.concatenate(
                [
                    jnp.concatenate(
                        [
                            now[i, n * 256 + a * 128 : n * 256 + (a + 1) * 128, :].T
                            for a in range(2)
                        ],
                        axis=1,
                    )
                    for i in range(IB)
                ],
                axis=0,
            )
            acc_t[:, n * 256 : (n + 1) * 256] += jnp.dot(
                cot, turned, preferred_element_type=F32
            )

        for n in range(4):
            for b in range(4 * n, 4 * n + 2):
                intermediate_tile(lt, w2_ref, later, b)
            right_of(n)
            for b in range(4 * n + 2, 4 * n + 4):
                intermediate_tile(lt, w2_ref, later, b)
            pair_of(n)

    @pl.when(g == pl.num_programs(0) - 1)
    def _():
        for b in range(8):
            acc[b * 128 : (b + 1) * 128, :] = acc_t[:, b * 128 : (b + 1) * 128].T
        for s in range(S):
            dr_ref[s // 2, (s % 2) * C : (s % 2 + 1) * C, :] = acc[
                pl.ds(s, C, stride=S), :
            ].astype(BF16)


def pairs(lt, rt, w2, bias, cot):
    whole = lambda shape: pl.BlockSpec(shape, lambda g: (0,) * len(shape))
    step = pl.BlockSpec((2 * IB, T, K), lambda g: (g, 0, 0))
    return pl.pallas_call(
        pair_kernel,
        grid=(T // (2 * IB),),
        out_shape=(
            jax.ShapeDtypeStruct((T, T, K), BF16),
            jax.ShapeDtypeStruct((N, 64, T), BF16),
        ),
        in_specs=[
            whole((T * S, C)),
            whole((C // 4, T, 4 * S)),
            whole((C, C, K)),
            whole((1, K)),
            step,
        ],
        out_specs=(step, whole((N, 64, T))),
        scratch_shapes=[
            pltpu.VMEM((IB, C * S, K), BF16),
            pltpu.VMEM((IB, C * S, K), BF16),
            pltpu.VMEM((T, C * S), F32),
            pltpu.VMEM((C * S, T), F32),
        ],
        compiler_params=pltpu.CompilerParams(
            dimension_semantics=("arbitrary",), vmem_limit_bytes=40 << 20
        ),
        name="pair_kernel",
    )(lt, rt, w2, bias, cot)


def total_of(blocks):
    total = blocks[0].astype(F32)
    for n in range(1, N):
        total += blocks[n].astype(F32)
    return total


def scatter_kernel(
    dr_ref, first_ref, wec_ref, rmat_ref, cot_hbm,
    gl_ref, gr_ref,
    dr_in, dl_in, dm_in, second, cot_buf, spread, sums, turned,
    cot_sem, rsend, rrecv, lsend, lrecv, msend, mrecv,
):
    me_w = lax.axis_index("wide")
    me_n = lax.axis_index("narrow")
    barrier = pltpu.get_barrier_semaphore()
    for t in range(HALF // IC):
        cot_copy(cot_hbm, cot_buf, cot_sem, HALF, t).start()
    greet(barrier, me_w, me_n)
    project_cotangent(HALF, (0, AHEAD), wec_ref, cot_hbm, cot_buf, cot_sem, spread)
    pl.semaphore_wait(barrier, 2 * (N - 1))

    def piece(blocks, me, d):
        return blocks.at[(me + d) % N]

    sends = [
        push("wide", me_w, d, piece(dr_ref, me_w, d), dr_in, rsend, rrecv) for d in NEAR_FIRST
    ]
    sends += [
        push("narrow", me_n, d, piece(first_ref, me_n, d), dl_in, lsend, lrecv)
        for d in NEAR_FIRST
    ]
    for copy in sends:
        copy.start()
    dr_in[me_w] = dr_ref[me_w]
    dl_in[me_n] = first_ref[me_n]

    project_cotangent(HALF, (AHEAD, HALF // IC), wec_ref, cot_hbm, cot_buf, cot_sem, spread)
    left_gradient(spread, rmat_ref, sums, lambda t: None)
    blocks_of(sums, turned, second)
    last = [
        push("narrow", me_n, d, piece(second, me_n, d), dm_in, msend, mrecv)
        for d in NEAR_FIRST[::-1]
    ]
    for copy in last:
        copy.start()
    dm_in[me_n] = second[me_n]

    for d in range(1, N):
        arrived("wide", me_w, d, piece(dr_ref, me_w, d), dr_in, rsend, rrecv)
    gr_ref[...] = total_of(dr_in)
    for d in range(1, N):
        arrived("narrow", me_n, d, piece(first_ref, me_n, d), dl_in, lsend, lrecv)
    one = total_of(dl_in)
    for copy in sends:
        copy.wait_send()
    for d in range(1, N):
        arrived("narrow", me_n, d, piece(second, me_n, d), dm_in, msend, mrecv)
    two = total_of(dm_in)
    for q in range(2):
        gl_ref[q * C : (q + 1) * C, :] = jnp.concatenate(
            [part[:, q * HALF : (q + 1) * HALF] for part in (one, two)], axis=1
        )
    for copy in last:
        copy.wait_send()


def scatter(dr, first, wec, rmat, cot):
    vmem = pl.BlockSpec(memory_space=pltpu.VMEM)
    return pl.pallas_call(
        scatter_kernel,
        out_shape=(
            jax.ShapeDtypeStruct((64, T), F32),
            jax.ShapeDtypeStruct((64, T), F32),
        ),
        in_specs=[vmem] * 4 + [pl.BlockSpec(memory_space=pltpu.HBM)],
        out_specs=(vmem, vmem),
        scratch_shapes=[
            pltpu.VMEM((N, 64, T), BF16),
            pltpu.VMEM((N, C, T), BF16),
            pltpu.VMEM((N, C, T), BF16),
            pltpu.VMEM((N, C, T), BF16),
            pltpu.VMEM((HALF, T, K), BF16),
            pltpu.VMEM((HALF, C, C, T), BF16),
            pltpu.VMEM((HALF * C, 128), F32),
            pltpu.VMEM((C * N, 128), F32),
            pltpu.SemaphoreType.DMA((HALF // IC,)),
        ]
        + [pltpu.SemaphoreType.DMA((N,))] * 6,
        compiler_params=pltpu.CompilerParams(
            collective_id=1, has_side_effects=True, vmem_limit_bytes=40 << 20
        ),
        name="scatter_kernel",
    )(dr, first, wec, rmat, pltpu.with_memory_space_constraint(cot, pltpu.HBM))


def local(left, right, out_weight, out_bias, cotangent):
    lt, rt, w2, wec, rmat, first = gather(
        left.reshape(64, T), right.reshape(64, T), out_weight, cotangent
    )
    pair_update, dr = pairs(lt, rt, w2, out_bias.reshape(1, K), cotangent)
    gl, gr = scatter(dr, first, wec, rmat, cotangent)
    return pair_update, gl.reshape(2, C, T), gr.reshape(2, C, T)


def solution(mesh):
    return jax.shard_map(
        local,
        mesh=mesh,
        in_specs=(
            P("narrow", None, "wide"),
            P("wide", None, "narrow"),
            P(),
            P(),
            P("wide", "narrow", None),
        ),
        out_specs=(P("wide", "narrow", None), P("narrow", None, "wide"), P("wide", None, "narrow")),
        check_vma=False,
    )
```

time: 303 us -> 69.3 us (0.23); the launches traced: 299 us -> 68.9 us
  local copies, waits for them, and re-layouts: 132 us -> 1.24 us
  matrix products: 99.1 us -> 0 us
  Pallas kernels: 0 us -> 66.9 us
  waiting for transfers between devices: 29.8 us -> 0 us
  starting transfers between devices: 19.2 us -> 0 us
  blocking collectives: 16.9 us -> 0 us
    dot_general x40 -> x0, matrix products: 99.1 us -> none  [the longest x8 38.4 us: block_step(): jnp.einsum('ijce,sci->sej', d_outer, left_block, preferred_element_type=j...]
    pallas_call x0 -> x3, Pallas kernels: none -> 66.9 us  [the longest x1 26.9 us: gather(): pl.pallas_call(gather_kernel, out_shape=(jax.ShapeDtypeStruct((T * S, C),...]
    convert_element_type x8 -> x0, local copies, waits for them, and re-layouts: 52.2 us -> none  [block_step(): d_outer.astype(jnp.bfloat16)]
    while x25 -> x0, local copies, waits for them, and re-layouts: 45.5 us -> none
    all_to_all x3 -> x0, waiting for transfers between devices: 29.8 us -> none  [the longest x2 22 us: summed_on_arrival(): lax.all_to_all(blocks, axis, split_axis=0, concat_axis=0, tiled=True)]
    all_to_all x3 -> x0, starting transfers between devices: 19.2 us -> none  [the longest x2 10.9 us: summed_on_arrival(): lax.all_to_all(blocks, axis, split_axis=0, concat_axis=0, tiled=True)]
    all_to_all x1 -> x0, blocking collectives: 16.9 us -> none  [copy_for_each(): return lax.all_to_all(copies, axis, split_axis=0, concat_axis=0, tiled=True)]
    dynamic_update_slice x8 -> x0, local copies, waits for them, and re-layouts: 15.3 us -> none  [block_step(): pairs = lax.dynamic_update_slice_in_dim(pairs, pair_out, start, 0)]
  transfers between devices with their start and end apart: 3 -> 0, of which waited for: 3 -> 0; matrix products, arithmetic and copies ran while one was open for 1% -> 0% of each run, Pallas kernels for 0% -> 0%
where the time goes in v2:
time: 69.3 us; the launch traced here: 68.9 us
  Pallas kernels  66.9 us (97%)
  local copies, waits for them, and re-layouts  1.24 us (2%)
    pallas_call x1, Pallas kernels, gather(): pl.pallas_call(gather_kernel, out_shape=(jax.ShapeDtypeStruct((T * S, C),...  26.9 us
    pallas_call x1, Pallas kernels, pairs(): pl.pallas_call(pair_kernel, grid=(T // (2 * IB),), out_shape=(jax.ShapeDt...  21.5 us
    pallas_call x1, Pallas kernels, scatter(): pl.pallas_call(scatter_kernel, out_shape=(jax.ShapeDtypeStruct((64, T), F...  18.5 us

profile of v2, /device:TPU:1, one launch (start us, length us, event | category | flops | bytes accessed | tf_op | source)
XLA Modules:
  0.0 68.9 jit_solution(10015548095283976036)
XLA Ops:
  0.6 0.0 copy-start
  0.6 0.0 copy-start.1
  0.7 26.9 %gather_kernel.1 = (bf16[4096,32]{1,0:T(8,128)(2,1)S(1)}, bf16[8,128,128]{2,1,0:T(8,128)(2,1)S(1)}, bf16[32,32,128]{2,1,0:T(8,128)(2,1)S(1)}, bf16[1024,128]{1,0...) custom-call(bf16[64,128]{1,0:T(8,128)(2,1)} %bitcast.8, bf16[64,128]{1,0:T(8,128)(2,1)} %bitcast.9, ...), custom_call_target="tpu_custom_call" | custom-call | tf_op jit(solution)/shard_map/gather_kernel/pallas_call | solution.py:172
  27.5 0.0 copy-done
  27.5 0.0 copy-done.1
  27.5 21.5 %pair_kernel.1 = (bf16[128,128,128]{2,1,0:T(8,128)(2,1)}, bf16[16,64,128]{2,1,0:T(8,128)(2,1)S(1)}) custom-call(bf16[4096,32]{1,0:T(8,128)(2,1)S(1)} %get-tuple-element.13.lt_ref, bf16[8,128,128]{2,1,0:T(8,128)(2,1)S(1)} %get-tuple-element.14.rt_ref, bf16[32,32,128]{2,1,0:T(8,128)(2,1)S(1)} %get-tuple-element.15.w2_ref, f32[1,128]{1,0:T(1,128)S(1)} %bitcast.7, ...), custom_call_target="tpu_custom_call" | custom-call | tf_op jit(solution)/shard_map/pair_kernel/pallas_call | solution.py:290
  49.1 18.5 %scatter_kernel.1 = (f32[64,128]{1,0:T(8,128)S(1)}, f32[64,128]{1,0:T(8,128)S(1)}) custom-call(bf16[16,64,128]{2,1,0:T(8,128)(2,1)S(1)} %get-tuple-element.17.dr_ref, bf16[16,32,128]{2,1,0:T(8,128)(2,1)S(1)} %get-tuple-element.18.first_ref, bf16[1024,128]{1,0:T(8,128)(2,1)S(1)} %get-tuple-element.19.wec_ref, ...), custom_call_target="tpu_custom_call" | custom-call | tf_op jit(solution)/shard_map/scatter_kernel/pallas_call | solution.py:387
  67.6 0.6 copy.10
  68.2 0.6 copy.11
Async XLA Ops:
  0.6 26.9 %copy-start = (bf16[128,128,128]{2,1,0:T(8,128)(2,1)S(1)}, bf16[128,128,128]{2,1,0:T(8,128)(2,1)}, u32[]{:S(2)}) copy-start(bf16[128,128,128]{2,1,0:T(8,128)(2,1)} %cot_hbm.3) | copy-start | bytes 12582916
  0.6 26.9 %copy-start.1 = (f32[128]{0:T(128)S(1)}, f32[128]{0:T(128)}, u32[]{:S(2)}) copy-start(f32[128]{0:T(128)} %param.8) | copy-start | bytes 1540

commit v3 on v0

v3 whole, which is shorter than its diff:
```python
import jax
import jax.numpy as jnp
from jax import lax
from jax.experimental import pallas as pl
from jax.experimental.pallas import tpu as pltpu
from jax.sharding import PartitionSpec as P

F32 = jnp.float32
BF16 = jnp.bfloat16
MESH = pl.DeviceIdType.MESH
NT = (((1,), (1,)), ((), ()))

N = 16
S = 32
C = 32
K = 128
T = 128
IC = 16
IM = 16
IB = 8
IP = 16
AHEAD = 4
LATE = 2
NEAR_FIRST = (1, 15, 8, 2, 14, 9, 7, 3, 13, 10, 6, 4, 12, 11, 5)


def push(axis, me, d, src, dst, send_sem, recv_sem):
    return pltpu.make_async_remote_copy(
        src, dst.at[me], send_sem.at[d], recv_sem.at[me],
        device_id={axis: (me + d) % N}, device_id_type=MESH,
    )


def arrived(axis, me, d, src, dst, send_sem, recv_sem):
    peer = (me + d) % N
    pltpu.make_async_remote_copy(
        src, dst.at[peer], send_sem.at[d], recv_sem.at[peer],
        device_id={axis: peer}, device_id_type=MESH,
    ).wait_recv()


def cot_copy(cot_hbm, cot_buf, sems, t):
    at = pl.multiple_of(t * IC, IC)
    return pltpu.make_async_copy(
        cot_hbm.at[pl.ds(at, IC)], cot_buf.at[pl.ds(at, IC)], sems.at[t]
    )


def total_of(blocks):
    total = blocks[0].astype(F32)
    for n in range(1, N):
        total += blocks[n].astype(F32)
    return total


def kernel(
    left_hbm, right_hbm, w_hbm, bias_hbm, cot_hbm,
    pair_ref, gl_ref, gr_ref,
    left_v, right_v, w_v, bias_v, l_buf, r_buf, cot_buf, wide_f, left_f, lt_f, lt, rt, w2, wec, rmat,
    big, sums, turned, acc_t, dl_out, dr_out, dl_in, dr_in,
    in_sem, cot_sem, lsend, lrecv, rsend, rrecv, dlsend, dlrecv, drsend, drrecv,
):
    me_w = lax.axis_index("wide")
    me_n = lax.axis_index("narrow")
    barrier = pltpu.get_barrier_semaphore()
    for d in range(1, N):
        pl.semaphore_signal(
            barrier, inc=1, device_id={"wide": (me_w + d) % N}, device_id_type=MESH
        )
        pl.semaphore_signal(
            barrier, inc=1, device_id={"narrow": (me_n + d) % N}, device_id_type=MESH
        )
    fetches = [
        pltpu.make_async_copy(src, dst, in_sem.at[n])
        for n, (src, dst) in enumerate(
            ((w_hbm, w_v), (right_hbm, right_v), (left_hbm, left_v), (bias_hbm, bias_v))
        )
    ]
    for copy in fetches:
        copy.start()
    for t in range(T // IC):
        cot_copy(cot_hbm, cot_buf, cot_sem, t).start()

    fetches[0].wait()
    wide_f[...] = w_v[...].astype(F32)
    for e in range(C):
        part = wide_f[pl.ds(e, C, stride=C), :].astype(BF16)
        w2[e] = part
        wec[e * C : (e + 1) * C, :] = part
    for copy in fetches[1:]:
        copy.wait()

    def project(t, _):
        cot_copy(cot_hbm, cot_buf, cot_sem, t).wait()
        base = t * IC
        for p in range(IC // 2):
            rows = cot_buf[pl.ds(base + 2 * p, 2)].reshape(2 * T, K)
            d = lax.dot_general(wec[...], rows, NT, preferred_element_type=F32)
            d = d.astype(BF16)
            for q in range(2):
                big[base + 2 * p + q] = d[:, q * T : (q + 1) * T]
        return 0

    lax.fori_loop(0, AHEAD, project, 0)
    pl.semaphore_wait(barrier, 2 * (N - 1))
    sends = [push("wide", me_w, d, right_v, r_buf, rsend, rrecv) for d in NEAR_FIRST]
    sends += [push("narrow", me_n, d, left_v, l_buf, lsend, lrecv) for d in NEAR_FIRST]
    for copy in sends:
        copy.start()
    r_buf[me_w] = right_v[...]
    l_buf[me_n] = left_v[...]
    lax.fori_loop(AHEAD, T // IC, project, 0)

    for d in range(1, N):
        arrived("wide", me_w, d, right_v, r_buf, rsend, rrecv)
    for w in range(N):
        wide_f[w * 64 : (w + 1) * 64, :] = r_buf[w].astype(F32)
    for e in range(C):
        rmat[e * T : (e + 1) * T, :] = wide_f[pl.ds(e, S, stride=C), :].T.astype(BF16)

    def left_gradient(t):
        rows = jnp.concatenate(
            [
                big[pl.ds(t * IM, IM), e * C : (e + 1) * C, :].reshape(IM * C, T)
                for e in range(C)
            ],
            axis=1,
        )
        out = jnp.dot(rows, rmat[...], preferred_element_type=F32)
        sums[pl.ds(pl.multiple_of(t * IM * C, IM * C), IM * C), 0:S] = out * (1.0 / S)

    def early(t, _):
        left_gradient(t)
        return 0

    def late(t, _):
        left_gradient(t)
        u = t - (T // IM - LATE)
        for q in range(S // LATE):
            s = u * (S // LATE) + q
            part = left_f[pl.ds(pl.multiple_of(s * C, C), C), :]
            lt_f[pl.ds(s, T, stride=S), 0:C] = part.T
        for q in range(8 // LATE):
            b = u * (8 // LATE) + q
            rows = jnp.concatenate(
                [wide_f[pl.ds(4 * b + m, S, stride=C), :] for m in range(4)], axis=0
            )
            rt[b] = rows.T.astype(BF16)
        return 0

    lax.fori_loop(0, T // IM - LATE, early, 0)
    for d in range(1, N):
        arrived("narrow", me_n, d, left_v, l_buf, lsend, lrecv)
    for n in range(N):
        left_f[n * 64 : (n + 1) * 64, :] = l_buf[n].astype(F32) * (1.0 / S)
    lax.fori_loop(T // IM - LATE, T // IM, late, 0)
    lt[...] = lt_f[:, 0:C].astype(BF16)

    for c in range(C):
        turned[c * S : (c + 1) * S, :] = sums[pl.ds(c, T, stride=C), :].T[0:S]
    for s in range(S):
        dl_out[s // 2, (s % 2) * C : (s % 2 + 1) * C, :] = turned[
            pl.ds(s, C, stride=S), :
        ].astype(BF16)
    dl_sends = [
        push("narrow", me_n, d, dl_out.at[(me_n + d) % N], dl_in, dlsend, dlrecv)
        for d in NEAR_FIRST
    ]
    for copy in dl_sends:
        copy.start()
    dl_in[me_n] = dl_out[me_n]

    def intermediate(chunk, b):
        rows = lt[pl.ds(pl.multiple_of(chunk * (IB * S), IB * S), IB * S), :]
        w = jnp.concatenate([w2[2 * b], w2[2 * b + 1]], axis=1)
        t = jnp.dot(rows, w, preferred_element_type=F32).astype(BF16)
        for i in range(IB):
            for q in range(2):
                e = 2 * b + q
                big[chunk * IB + i, e * S : (e + 1) * S, :] = t[
                    i * S : (i + 1) * S, q * K : (q + 1) * K
                ]

    def right_gradient(chunk, n):
        cot = jnp.concatenate([cot_buf[chunk * IB + i] for i in range(IB)], axis=1)
        back = jnp.concatenate(
            [
                jnp.concatenate(
                    [
                        big[
                            chunk * IB + i, n * 256 + a * 128 : n * 256 + (a + 1) * 128, :
                        ].T
                        for a in range(2)
                    ],
                    axis=1,
                )
                for i in range(IB)
            ],
            axis=0,
        )
        acc_t[:, n * 256 : (n + 1) * 256] += jnp.dot(cot, back, preferred_element_type=F32)

    def both(chunk):
        for n in range(4):
            for b in range(4 * n, 4 * n + 4):
                intermediate(chunk + 1, b)
            right_gradient(chunk, n)

    def two_chunks(g, _):
        both(2 * g)
        both(2 * g + 1)
        return 0

    acc_t[...] = jnp.zeros_like(acc_t)
    for b in range(C // 2):
        intermediate(0, b)
    last = T // IB - 2
    lax.fori_loop(0, last // 2, two_chunks, 0)
    both(last)
    for n in range(4):
        right_gradient(last + 1, n)

    for b in range(8):
        turned[b * 128 : (b + 1) * 128, :] = acc_t[:, b * 128 : (b + 1) * 128].T
    for s in range(S):
        dr_out[s // 2, (s % 2) * C : (s % 2 + 1) * C, :] = turned[
            pl.ds(s, C, stride=S), :
        ].astype(BF16)
    dr_sends = [
        push("wide", me_w, d, dr_out.at[(me_w + d) % N], dr_in, drsend, drrecv)
        for d in NEAR_FIRST
    ]
    for copy in dr_sends:
        copy.start()
    dr_in[me_w] = dr_out[me_w]

    def pairs(t, _):
        rows = jnp.concatenate([rt[b] for b in range(8)], axis=1)
        for p in range(IP // 2):
            i = t * IP + 2 * p
            cols = jnp.concatenate([big[i], big[i + 1]], axis=1)
            out = jnp.dot(rows, cols, preferred_element_type=F32)
            for q in range(2):
                pair_ref[i + q] = (out[:, q * K : (q + 1) * K] + bias_v[...]).astype(BF16)
        return 0

    lax.fori_loop(0, T // IP, pairs, 0)

    for d in range(1, N):
        arrived("narrow", me_n, d, dl_out.at[0], dl_in, dlsend, dlrecv)
    gl_ref[...] = total_of(dl_in)
    for copy in sends + dl_sends:
        copy.wait_send()
    for d in range(1, N):
        arrived("wide", me_w, d, dr_out.at[0], dr_in, drsend, drrecv)
    gr_ref[...] = total_of(dr_in)
    for copy in dr_sends:
        copy.wait_send()


def local(left, right, out_weight, out_bias, cotangent):
    vmem = pl.BlockSpec(memory_space=pltpu.VMEM)
    hbm = pl.BlockSpec(memory_space=pltpu.HBM)
    pin = lambda x: pltpu.with_memory_space_constraint(x, pltpu.HBM)
    pair_update, gl, gr = pl.pallas_call(
        kernel,
        out_shape=(
            jax.ShapeDtypeStruct((T, T, K), BF16),
            jax.ShapeDtypeStruct((64, T), F32),
            jax.ShapeDtypeStruct((64, T), F32),
        ),
        in_specs=[hbm] * 5,
        out_specs=(vmem,) * 3,
        scratch_shapes=[
            pltpu.VMEM((64, T), BF16),
            pltpu.VMEM((64, T), BF16),
            pltpu.VMEM((C * C, K), BF16),
            pltpu.VMEM((1, K), F32),
            pltpu.VMEM((N, 64, T), BF16),
            pltpu.VMEM((N, 64, T), BF16),
            pltpu.VMEM((T, T, K), BF16),
            pltpu.VMEM((C * S, 128), F32),
            pltpu.VMEM((C * S, 128), F32),
            pltpu.VMEM((T * S, 128), F32),
            pltpu.VMEM((T * S, C), BF16),
            pltpu.VMEM((8, T, 128), BF16),
            pltpu.VMEM((C, C, K), BF16),
            pltpu.VMEM((C * C, K), BF16),
            pltpu.VMEM((C * T, S), BF16),
            pltpu.VMEM((T, C * S, 128), BF16),
            pltpu.VMEM((T * C, 128), F32),
            pltpu.VMEM((C * S, 128), F32),
            pltpu.VMEM((T, C * S), F32),
            pltpu.VMEM((N, 64, T), BF16),
            pltpu.VMEM((N, 64, T), BF16),
            pltpu.VMEM((N, 64, T), BF16),
            pltpu.VMEM((N, 64, T), BF16),
            pltpu.SemaphoreType.DMA((4,)),
            pltpu.SemaphoreType.DMA((T // IC,)),
        ]
        + [pltpu.SemaphoreType.DMA((N,))] * 8,
        compiler_params=pltpu.CompilerParams(
            collective_id=0, has_side_effects=True, vmem_limit_bytes=49 << 20
        ),
        name="outer_product_mean",
    )(
        pin(left.reshape(64, T)),
        pin(right.reshape(64, T)),
        pin(out_weight),
        pin(out_bias.reshape(1, K)),
        pin(cotangent),
    )
    return pair_update, gl.reshape(2, C, T), gr.reshape(2, C, T)


def solution(mesh):
    return jax.shard_map(
        local,
        mesh=mesh,
        in_specs=(
            P("narrow", None, "wide"),
            P("wide", None, "narrow"),
            P(),
            P(),
            P("wide", "narrow", None),
        ),
        out_specs=(P("wide", "narrow", None), P("narrow", None, "wide"), P("wide", None, "narrow")),
        check_vma=False,
    )
```

time: 303 us -> 58.6 us (0.19); the launches traced: 299 us -> 57.6 us
  local copies, waits for them, and re-layouts: 132 us -> 3.24 us
  matrix products: 99.1 us -> 0 us
  Pallas kernels: 0 us -> 53.7 us
  waiting for transfers between devices: 29.8 us -> 0 us
  starting transfers between devices: 19.2 us -> 0 us
  blocking collectives: 16.9 us -> 0 us
    dot_general x40 -> x0, matrix products: 99.1 us -> none  [the longest x8 38.4 us: block_step(): jnp.einsum('ijce,sci->sej', d_outer, left_block, preferred_element_type=j...]
    pallas_call x0 -> x1, Pallas kernels: none -> 53.7 us  [local(): pl.pallas_call(kernel, out_shape=(jax.ShapeDtypeStruct((T, T, K), BF16),...]
    convert_element_type x8 -> x0, local copies, waits for them, and re-layouts: 52.2 us -> none  [block_step(): d_outer.astype(jnp.bfloat16)]
    while x25 -> x0, local copies, waits for them, and re-layouts: 45.5 us -> none
    all_to_all x3 -> x0, waiting for transfers between devices: 29.8 us -> none  [the longest x2 22 us: summed_on_arrival(): lax.all_to_all(blocks, axis, split_axis=0, concat_axis=0, tiled=True)]
    all_to_all x3 -> x0, starting transfers between devices: 19.2 us -> none  [the longest x2 10.9 us: summed_on_arrival(): lax.all_to_all(blocks, axis, split_axis=0, concat_axis=0, tiled=True)]
    all_to_all x1 -> x0, blocking collectives: 16.9 us -> none  [copy_for_each(): return lax.all_to_all(copies, axis, split_axis=0, concat_axis=0, tiled=True)]
    dynamic_update_slice x8 -> x0, local copies, waits for them, and re-layouts: 15.3 us -> none  [block_step(): pairs = lax.dynamic_update_slice_in_dim(pairs, pair_out, start, 0)]
  transfers between devices with their start and end apart: 3 -> 0, of which waited for: 3 -> 0; matrix products, arithmetic and copies ran while one was open for 1% -> 0% of each run, Pallas kernels for 0% -> 0%
where the time goes in v3:
time: 58.6 us; the launch traced here: 57.6 us
  Pallas kernels  53.7 us (92%)
  local copies, waits for them, and re-layouts  3.24 us (6%)
  between operations  0.64 us (1%)
    pallas_call x1, Pallas kernels, local(): pl.pallas_call(kernel, out_shape=(jax.ShapeDtypeStruct((T, T, K), BF16),...  53.7 us
    unnamed x3, local copies, waits for them, and re-layouts  3.24 us

profile of v3, /device:TPU:1, one launch (start us, length us, event | category | flops | bytes accessed | tf_op | source)
XLA Modules:
  0.0 57.6 jit_solution(4498090583806791437)
XLA Ops:
  0.6 53.7 %outer_product_mean.1 = (bf16[128,128,128]{2,1,0:T(8,128)(2,1)S(1)}, f32[64,128]{1,0:T(8,128)S(1)}, f32[64,128]{1,0:T(8,128)S(1)}) custom-call(bf16[64,128]{1,0:T(8,128)(2,1)} %bitcast.7, bf16[64,128]{1,0:T(8,128)(2,1)} %bitcast.8, bf16[1024,128]{1,0:T(8,128)(2,1)} %w_hbm.1, f32[1,128]{1,0:T(1,128)} %bitcast.9, bf16[128,128,128]{2,1,0:T(8,128)(2,1)} %cot_hbm.1), custom_call_target="tpu_custom_call" | custom-call | tf_op jit(solution)/shard_map/outer_product_mean/pallas_call | solution.py:265
  54.4 2.0 %copy.11 = bf16[128,128,128]{2,1,0:T(8,128)(2,1)} copy(bf16[128,128,128]{2,1,0:T(8,128)(2,1)S(1)} %get-tuple-element.12) | data formatting | bytes 8388608
  56.4 0.6 %copy.12 = f32[2,32,128]{2,1,0:T(8,128)} copy(f32[2,32,128]{2,1,0:T(8,128)S(1)} %bitcast.6) | data formatting | bytes 65536
  57.0 0.6 %copy.13 = f32[2,32,128]{2,1,0:T(8,128)} copy(f32[2,32,128]{2,1,0:T(8,128)S(1)} %bitcast.5) | data formatting | bytes 65536

commit v4 on v3

--- a/solution.py
+++ b/solution.py
@@ -16,7 +16,8 @@
 K = 128
 T = 128
 IC = 16
-IM = 16
+IM = 4
+GAP = T + 8
 IB = 8
 IP = 16
 AHEAD = 4
@@ -55,9 +56,9 @@
 
 def kernel(
     left_hbm, right_hbm, w_hbm, bias_hbm, cot_hbm,
-    pair_ref, gl_ref, gr_ref,
-    left_v, right_v, w_v, bias_v, l_buf, r_buf, cot_buf, wide_f, left_f, lt_f, lt, rt, w2, wec, rmat,
-    big, sums, turned, acc_t, dl_out, dr_out, dl_in, dr_in,
+    pair_ref, dl_in, dr_in,
+    left_v, right_v, w_v, bias_v, l_buf, r_buf, cot_buf, wide_f, left_f, lt_f, lt, rt, w2,
+    big, right_l, turned, acc_t, dl_out, dr_out,
     in_sem, cot_sem, lsend, lrecv, rsend, rrecv, dlsend, dlrecv, drsend, drrecv,
 ):
     me_w = lax.axis_index("wide")
@@ -81,21 +82,25 @@
     for t in range(T // IC):
         cot_copy(cot_hbm, cot_buf, cot_sem, t).start()
 
-    fetches[0].wait()
-    wide_f[...] = w_v[...].astype(F32)
-    for e in range(C):
-        part = wide_f[pl.ds(e, C, stride=C), :].astype(BF16)
-        w2[e] = part
-        wec[e * C : (e + 1) * C, :] = part
-    for copy in fetches[1:]:
+    def turn(t, _):
+        cot_copy(cot_hbm, cot_buf, cot_sem, t).wait()
+        for i in range(IC):
+            lt_f[i * GAP : i * GAP + T, :] = cot_buf[t * IC + i].astype(F32)
+        for j in range(T):
+            pair_ref[j, pl.ds(pl.multiple_of(t * IC, IC), IC), :] = lt_f[
+                pl.ds(j, IC, stride=GAP), :
+            ].astype(BF16)
+        return 0
+
+    lax.fori_loop(0, T // IC, turn, 0)
+    for copy in fetches:
         copy.wait()
 
     def project(t, _):
-        cot_copy(cot_hbm, cot_buf, cot_sem, t).wait()
         base = t * IC
         for p in range(IC // 2):
-            rows = cot_buf[pl.ds(base + 2 * p, 2)].reshape(2 * T, K)
-            d = lax.dot_general(wec[...], rows, NT, preferred_element_type=F32)
+            rows = pair_ref[pl.ds(base + 2 * p, 2)].reshape(2 * T, K)
+            d = lax.dot_general(w_v[...], rows, NT, preferred_element_type=F32)
             d = d.astype(BF16)
             for q in range(2):
                 big[base + 2 * p + q] = d[:, q * T : (q + 1) * T]
@@ -111,23 +116,39 @@
     l_buf[me_n] = left_v[...]
     lax.fori_loop(AHEAD, T // IC, project, 0)
 
+    wide_f[...] = w_v[...].astype(F32)
+    for e in range(C):
+        w2[e] = wide_f[pl.ds(e, C, stride=C), :].astype(BF16)
+
     for d in range(1, N):
         arrived("wide", me_w, d, right_v, r_buf, rsend, rrecv)
     for w in range(N):
         wide_f[w * 64 : (w + 1) * 64, :] = r_buf[w].astype(F32)
-    for e in range(C):
-        rmat[e * T : (e + 1) * T, :] = wide_f[pl.ds(e, S, stride=C), :].T.astype(BF16)
+    for s in range(S):
+        lt_f[s * T : (s + 1) * T, 0:C] = wide_f[s * C : (s + 1) * C, :].T
+    for s in range(S):
+        turned[s * 32 : (s + 1) * 32, :] = jnp.concatenate(
+            [lt_f[pl.ds(s * T + m, 32, stride=4), 0:C] for m in range(4)], axis=1
+        )
+    for b in range(T // 4):
+        right_l[b] = turned[pl.ds(b, S, stride=32), :].astype(BF16)
 
     def left_gradient(t):
-        rows = jnp.concatenate(
-            [
-                big[pl.ds(t * IM, IM), e * C : (e + 1) * C, :].reshape(IM * C, T)
-                for e in range(C)
-            ],
-            axis=1,
-        )
-        out = jnp.dot(rows, rmat[...], preferred_element_type=F32)
-        sums[pl.ds(pl.multiple_of(t * IM * C, IM * C), IM * C), 0:S] = out * (1.0 / S)
+        rows = jnp.concatenate([right_l[b] for b in range(T // 4)], axis=1)
+        for p in range(IM // 2):
+            c = t * IM + 2 * p
+            cols = jnp.concatenate(
+                [
+                    big[:, pl.ds(pl.multiple_of((c + q) * C, C), C), :].reshape(T * C, T)
+                    for q in range(2)
+                ],
+                axis=1,
+            )
+            out = jnp.dot(rows, cols, preferred_element_type=F32) * (1.0 / S)
+            for q in range(2):
+                turned[pl.ds(pl.multiple_of((c + q) * S, S), S), :] = out[
+                    :, q * T : (q + 1) * T
+                ]
 
     def early(t, _):
         left_gradient(t)
@@ -135,7 +156,7 @@
 
     def late(t, _):
         left_gradient(t)
-        u = t - (T // IM - LATE)
+        u = t - (C // IM - LATE)
         for q in range(S // LATE):
             s = u * (S // LATE) + q
             part = left_f[pl.ds(pl.multiple_of(s * C, C), C), :]
@@ -148,16 +169,14 @@
             rt[b] = rows.T.astype(BF16)
         return 0
 
-    lax.fori_loop(0, T // IM - LATE, early, 0)
+    lax.fori_loop(0, C // IM - LATE, early, 0)
     for d in range(1, N):
         arrived("narrow", me_n, d, left_v, l_buf, lsend, lrecv)
     for n in range(N):
         left_f[n * 64 : (n + 1) * 64, :] = l_buf[n].astype(F32) * (1.0 / S)
-    lax.fori_loop(T // IM - LATE, T // IM, late, 0)
+    lax.fori_loop(C // IM - LATE, C // IM, late, 0)
     lt[...] = lt_f[:, 0:C].astype(BF16)
 
-    for c in range(C):
-        turned[c * S : (c + 1) * S, :] = sums[pl.ds(c, T, stride=C), :].T[0:S]
     for s in range(S):
         dl_out[s // 2, (s % 2) * C : (s % 2 + 1) * C, :] = turned[
             pl.ds(s, C, stride=S), :
@@ -248,26 +267,44 @@
 
     for d in range(1, N):
         arrived("narrow", me_n, d, dl_out.at[0], dl_in, dlsend, dlrecv)
-    gl_ref[...] = total_of(dl_in)
     for copy in sends + dl_sends:
         copy.wait_send()
     for d in range(1, N):
         arrived("wide", me_w, d, dr_out.at[0], dr_in, drsend, drrecv)
-    gr_ref[...] = total_of(dr_in)
     for copy in dr_sends:
         copy.wait_send()
+
+
+def finish_kernel(
+    pair_v, dl_in, dr_in, pair_hbm, gl_hbm, gr_hbm, gl_v, gr_v, sems
+):
+    part = T // 4
+    copies = [
+        pltpu.make_async_copy(
+            pair_v.at[pl.ds(n * part, part)], pair_hbm.at[pl.ds(n * part, part)], sems.at[n]
+        )
+        for n in range(4)
+    ]
+    for copy in copies:
+        copy.start()
+    for blocks, total, out, n in ((dl_in, gl_v, gl_hbm, 4), (dr_in, gr_v, gr_hbm, 5)):
+        total[...] = total_of(blocks).reshape(2, C, T)
+        copies.append(pltpu.make_async_copy(total, out, sems.at[n]))
+        copies[-1].start()
+    for copy in copies:
+        copy.wait()
 
 
 def local(left, right, out_weight, out_bias, cotangent):
     vmem = pl.BlockSpec(memory_space=pltpu.VMEM)
     hbm = pl.BlockSpec(memory_space=pltpu.HBM)
     pin = lambda x: pltpu.with_memory_space_constraint(x, pltpu.HBM)
-    pair_update, gl, gr = pl.pallas_call(
+    pair_v, dl, dr = pl.pallas_call(
         kernel,
         out_shape=(
             jax.ShapeDtypeStruct((T, T, K), BF16),
-            jax.ShapeDtypeStruct((64, T), F32),
-            jax.ShapeDtypeStruct((64, T), F32),
+            jax.ShapeDtypeStruct((N, 64, T), BF16),
+            jax.ShapeDtypeStruct((N, 64, T), BF16),
         ),
         in_specs=[hbm] * 5,
         out_specs=(vmem,) * 3,
@@ -285,14 +322,10 @@
             pltpu.VMEM((T * S, C), BF16),
             pltpu.VMEM((8, T, 128), BF16),
             pltpu.VMEM((C, C, K), BF16),
-            pltpu.VMEM((C * C, K), BF16),
-            pltpu.VMEM((C * T, S), BF16),
             pltpu.VMEM((T, C * S, 128), BF16),
-            pltpu.VMEM((T * C, 128), F32),
+            pltpu.VMEM((T // 4, S, 128), BF16),
             pltpu.VMEM((C * S, 128), F32),
             pltpu.VMEM((T, C * S), F32),
-            pltpu.VMEM((N, 64, T), BF16),
-            pltpu.VMEM((N, 64, T), BF16),
             pltpu.VMEM((N, 64, T), BF16),
             pltpu.VMEM((N, 64, T), BF16),
             pltpu.SemaphoreType.DMA((4,)),
@@ -310,7 +343,23 @@
         pin(out_bias.reshape(1, K)),
         pin(cotangent),
     )
-    return pair_update, gl.reshape(2, C, T), gr.reshape(2, C, T)
+    return pl.pallas_call(
+        finish_kernel,
+        out_shape=(
+            jax.ShapeDtypeStruct((T, T, K), BF16),
+            jax.ShapeDtypeStruct((2, C, T), F32),
+            jax.ShapeDtypeStruct((2, C, T), F32),
+        ),
+        in_specs=[vmem] * 3,
+        out_specs=(hbm,) * 3,
+        scratch_shapes=[
+            pltpu.VMEM((2, C, T), F32),
+            pltpu.VMEM((2, C, T), F32),
+            pltpu.SemaphoreType.DMA((6,)),
+        ],
+        compiler_params=pltpu.CompilerParams(vmem_limit_bytes=4 << 20),
+        name="finish",
+    )(pair_v, dl, dr)
 
 
 def solution(mesh):

time: 58.6 us -> 54.5 us (0.930)
  local copies, waits for them, and re-layouts: 3.24 us -> 0 us
    unnamed x3 -> x0, local copies, waits for them, and re-layouts: 3.24 us -> none
    pallas_call x1, Pallas kernels: 53.7 us -> 51.2 us  [local(): pl.pallas_call(kernel, out_shape=(jax.ShapeDtypeStruct((T, T, K), BF16),...]
    pallas_call x0 -> x1, Pallas kernels: none -> 2.06 us  [local(): pl.pallas_call(finish_kernel, out_shape=(jax.ShapeDtypeStruct((T, T, K),...]
where the time goes in v4:
time: 54.5 us; the launch traced here: 53.9 us
  Pallas kernels  53.2 us (98%)
  between operations  0.64 us (1%)
    pallas_call x1, Pallas kernels, local(): pl.pallas_call(kernel, out_shape=(jax.ShapeDtypeStruct((T, T, K), BF16),...  51.2 us
    pallas_call x1, Pallas kernels, local(): pl.pallas_call(finish_kernel, out_shape=(jax.ShapeDtypeStruct((T, T, K),...  2.06 us

profile of v4, /device:TPU:1, one launch (start us, length us, event | category | flops | bytes accessed | tf_op | source)
XLA Modules:
  0.0 53.9 jit_solution(14879436015737319629)
XLA Ops:
  0.6 51.2 %outer_product_mean.1 = (bf16[128,128,128]{2,1,0:T(8,128)(2,1)S(1)}, bf16[16,64,128]{2,1,0:T(8,128)(2,1)S(1)}, bf16[16,64,128]{2,1,0:T(8,128)(2,1)S(1)}) custom-call(bf16[64,128]{1,0:T(8,128)(2,1)} %bitcast.3, bf16[64,128]{1,0:T(8,128)(2,1)} %bitcast.4, bf16[1024,128]{1,0:T(8,128)(2,1)} %w_hbm.1, f32[1,128]{1,0:T(1,128)} %bitcast.5, ...), custom_call_target="tpu_custom_call" | custom-call | tf_op jit(solution)/shard_map/outer_product_mean/pallas_call | solution.py:302
  51.8 2.1 %finish.1 = (bf16[128,128,128]{2,1,0:T(8,128)(2,1)}, f32[2,32,128]{2,1,0:T(8,128)}, f32[2,32,128]{2,1,0:T(8,128)}) custom-call(bf16[128,128,128]{2,1,0:T(8,128)(2,1)S(1)} %get-tuple-element.6.pair_v, bf16[16,64,128]{2,1,0:T(8,128)(2,1)S(1)} %get-tuple-element.7.dl_in, bf16[16,64,128]{2,1,0:T(8,128)(2,1)S(1)} %get-tuple-element.8.dr_in), custom_call_target="tpu_custom_call" | custom-call | tf_op jit(solution)/shard_map/finish/pallas_call | solution.py:346

commit v5 on v4

--- a/solution.py
+++ b/solution.py
@@ -20,7 +20,7 @@
 GAP = T + 8
 IB = 8
 IP = 16
-AHEAD = 4
+AHEAD = 2
 LATE = 2
 NEAR_FIRST = (1, 15, 8, 2, 14, 9, 7, 3, 13, 10, 6, 4, 12, 11, 5)
 

time: 54.5 us -> 54.2 us (level)
  no operation moved by 1% of the time
where the time goes in v5:
time: 54.2 us; the launch traced here: 54.1 us
  Pallas kernels  53.4 us (99%)
  between operations  0.64 us (1%)
    pallas_call x1, Pallas kernels, local(): pl.pallas_call(kernel, out_shape=(jax.ShapeDtypeStruct((T, T, K), BF16),...  51.4 us
    pallas_call x1, Pallas kernels, local(): pl.pallas_call(finish_kernel, out_shape=(jax.ShapeDtypeStruct((T, T, K),...  2.06 us

profile of v5, /device:TPU:1, one launch (start us, length us, event | category | flops | bytes accessed | tf_op | source)
XLA Modules:
  0.0 54.1 jit_solution(10205597078286292508)
XLA Ops:
  0.6 51.4 %outer_product_mean.1 = (bf16[128,128,128]{2,1,0:T(8,128)(2,1)S(1)}, bf16[16,64,128]{2,1,0:T(8,128)(2,1)S(1)}, bf16[16,64,128]{2,1,0:T(8,128)(2,1)S(1)}) custom-call(bf16[64,128]{1,0:T(8,128)(2,1)} %bitcast.3, bf16[64,128]{1,0:T(8,128)(2,1)} %bitcast.4, bf16[1024,128]{1,0:T(8,128)(2,1)} %w_hbm.1, f32[1,128]{1,0:T(1,128)} %bitcast.5, ...), custom_call_target="tpu_custom_call" | custom-call | tf_op jit(solution)/shard_map/outer_product_mean/pallas_call | solution.py:302
  52.0 2.1 %finish.1 = (bf16[128,128,128]{2,1,0:T(8,128)(2,1)}, f32[2,32,128]{2,1,0:T(8,128)}, f32[2,32,128]{2,1,0:T(8,128)}) custom-call(bf16[128,128,128]{2,1,0:T(8,128)(2,1)S(1)} %get-tuple-element.6.pair_v, bf16[16,64,128]{2,1,0:T(8,128)(2,1)S(1)} %get-tuple-element.7.dl_in, bf16[16,64,128]{2,1,0:T(8,128)(2,1)S(1)} %get-tuple-element.8.dr_in), custom_call_target="tpu_custom_call" | custom-call | tf_op jit(solution)/shard_map/finish/pallas_call | solution.py:346
